TPU v7x, 32 devices: a whole 2x2x4 slice. The times are simulated.
32 devices in a mesh: row: 8 (over y, x, core), col: 4 (over z).
Axes of the slice: x: 2, y: 2, z: 4, core: 2. Of those that a mesh axis runs over, the one named last changes fastest.
Arguments:
- value_proj: float32 [8, 4, 1024, 512], P('row', 'col'), may hold values from -6 to 6
- token_pool: bfloat16 [8, 4, 1536, 1024], P('row', 'col'), may hold values from -6 to 6
- target_pool: bfloat16 [8, 4, 1536, 1024], P('row', 'col'), may hold values from -6 to 6
- batch_ids: int32 [8, 4, 3, 1536], P('row', 'col'), may hold values from 0 to 1535
- frozen_out: bfloat16 [512, 1024], replicated, may hold values from -0.25 to 0.25
- numerators: int32 [3], replicated, may hold values from 4 to 15
Outputs:
- final_proj: float32 [8, 4, 1024, 512], P('row', 'col')
- final_tracker: float32 [8, 4, 1024, 512], P('row', 'col')
All inputs are finite; a program needn't handle non-finite values.
Results may differ from a plain program's by a relative error of at most 0.017.
Values sent between devices are 32-bit elements; how exact they have to be, the bound alone decides.
No kernel may reach another device: no remote copies, remote signals or barrier semaphores. Data moves between devices by JAX's collectives and lax.ppermute only.
A program may use at most 128 MiB of HBM per device.

v0:
```python
import functools

import jax
import jax.numpy as jnp
from jax import lax
from jax.experimental import pallas as pl
from jax.experimental.pallas import tpu as pltpu
from jax.sharding import PartitionSpec as P


ITERS = 2

step_rate = 0.2


def shifted(block, axis, distance):
    devices = range(lax.axis_size(axis))
    route = [((i - distance) % len(devices), i) for i in devices]
    return lax.ppermute(block, axis, route)


def tile_of(rows, most):
    tile = min(rows, most)
    while rows % tile:
        tile -= 8
    return tile


def gradient_body(which, tile, factor, ids_ref, x_ref, tok_ref, tgt_ref, out_ref, g_ref, xb_ref):
    step = pl.program_id(0)

    @pl.when(step == 0)
    def _():
        xb_ref[...] = x_ref[...].astype(jnp.bfloat16)

    tokens = tok_ref[...]
    frozen = out_ref[...]
    preact = jnp.dot(tokens, xb_ref[...], preferred_element_type=jnp.float32) * factor
    sigmoid_pre = jax.nn.sigmoid(preact)
    hidden = (preact * sigmoid_pre).astype(jnp.bfloat16)
    output = jnp.dot(hidden, frozen, preferred_element_type=jnp.float32)
    error_term = (output - tgt_ref[...].astype(jnp.float32)).astype(jnp.bfloat16)
    back_hidden = lax.dot_general(
        error_term, frozen, (((1,), (1,)), ((), ())), preferred_element_type=jnp.float32
    )
    slope = sigmoid_pre * (1.0 + preact * (1.0 - sigmoid_pre))
    rows = lax.broadcasted_iota(jnp.int32, (tile, ids_ref.shape[1]), 0) + step * tile
    named = jnp.where(rows == ids_ref[which : which + 1, :], 1.0, 0.0)
    times = jnp.sum(named, axis=1, keepdims=True)
    back_pre = (back_hidden * slope * times).astype(jnp.bfloat16)
    part = factor * lax.dot_general(
        tokens, back_pre, (((0,), (0,)), ((), ())), preferred_element_type=jnp.float32
    )

    @pl.when(step == 0)
    def _():
        g_ref[...] = part

    @pl.when(step > 0)
    def _():
        g_ref[...] += part


def local_gradient(which, current, tokens, targets, ids, frozen_out):
    pool, width = tokens.shape
    heads = current.shape[1]
    tile = tile_of(pool, 512)
    whole = lambda shape: pl.BlockSpec(shape, lambda i: (0, 0))
    return pl.pallas_call(
        functools.partial(gradient_body, which, tile, width ** (-0.5)),
        grid=(pool // tile,),
        in_specs=[
            whole(ids.shape),
            whole(current.shape),
            pl.BlockSpec((tile, width), lambda i: (i, 0)),
            pl.BlockSpec((tile, width), lambda i: (i, 0)),
            whole(frozen_out.shape),
        ],
        out_specs=whole((width, heads)),
        out_shape=jax.ShapeDtypeStruct((width, heads), jnp.float32),
        scratch_shapes=[pltpu.VMEM(current.shape, jnp.bfloat16)],
        compiler_params=pltpu.CompilerParams(
            dimension_semantics=("arbitrary",), vmem_limit_bytes=32 * 2**20
        ),
        cost_estimate=pl.CostEstimate(
            flops=8 * pool * width * heads, bytes_accessed=12 * 2**20, transcendentals=0
        ),
    )(ids, current, tokens, targets, frozen_out)


def add_body(weight_ref, rest_ref, piece_ref, out_ref):
    out_ref[...] = rest_ref[...] + weight_ref[0] * piece_ref[...]


def add_piece(weight, rest, piece, start):
    rows, heads = piece.shape
    tile = tile_of(rows, 128)
    first = start // tile
    return pl.pallas_call(
        add_body,
        grid=(rows // tile,),
        in_specs=[
            pl.BlockSpec(memory_space=pltpu.SMEM),
            pl.BlockSpec((tile, heads), lambda i: (i + first, 0)),
            pl.BlockSpec((tile, heads), lambda i: (i, 0)),
        ],
        out_specs=pl.BlockSpec((tile, heads), lambda i: (i + first, 0)),
        out_shape=jax.ShapeDtypeStruct(rest.shape, rest.dtype),
        input_output_aliases={1: 0},
        compiler_params=pltpu.CompilerParams(vmem_limit_bytes=4 * 2**20),
        cost_estimate=pl.CostEstimate(
            flops=2 * rows * heads, bytes_accessed=12 * rows * heads, transcendentals=0
        ),
        name="add_piece",
    )(weight, rest, piece)


def tail_body(start, weight_ref, filled_ref, rest_ref, piece_ref, out_ref, sum_ref, sem):
    sum_ref[...] = rest_ref[...] + weight_ref[0] * piece_ref[...]
    copy = pltpu.make_async_copy(sum_ref, out_ref.at[pl.ds(start, sum_ref.shape[0])], sem)
    copy.start()
    copy.wait()


def add_tail(weight, filled, rest, piece, start):
    rows, heads = piece.shape
    return pl.pallas_call(
        functools.partial(tail_body, start),
        in_specs=[
            pl.BlockSpec(memory_space=pltpu.SMEM),
            pl.BlockSpec(memory_space=pl.ANY),
            pl.BlockSpec(memory_space=pltpu.VMEM),
            pl.BlockSpec(memory_space=pltpu.VMEM),
        ],
        out_specs=pl.BlockSpec(memory_space=pl.ANY),
        out_shape=jax.ShapeDtypeStruct(filled.shape, filled.dtype),
        scratch_shapes=[pltpu.VMEM(piece.shape, piece.dtype), pltpu.SemaphoreType.DMA],
        input_output_aliases={1: 0},
        compiler_params=pltpu.CompilerParams(vmem_limit_bytes=4 * 2**20),
        cost_estimate=pl.CostEstimate(
            flops=2 * rows * heads, bytes_accessed=12 * rows * heads, transcendentals=0
        ),
        name="add_tail",
    )(weight, filled, rest, piece)


def track_body(spans, w_ref, own_ref, row_ref, col_ref, new_ref, old_ref, all_ref, *piece_refs):
    step = pl.program_id(0)
    mixed = w_ref[0] * own_ref[...] + w_ref[1] * row_ref[...] + w_ref[2] * col_ref[...]
    tracker = mixed + new_ref[...] - old_ref[...]
    all_ref[...] = tracker
    for (first, end), piece_ref in zip(spans, piece_refs):

        @pl.when((step >= first) & (step < end))
        def _():
            piece_ref[...] = tracker


def near_body(spans, w_ref, own_ref, row_ref, new_ref, old_ref, all_ref, *piece_refs):
    step = pl.program_id(0)
    near = w_ref[0] * own_ref[...] + w_ref[1] * row_ref[...] + (new_ref[...] - old_ref[...])
    all_ref[...] = near
    for (first, end), piece_ref in zip(spans, piece_refs):

        @pl.when((step >= first) & (step < end))
        def _():
            piece_ref[...] = near


def sweep(body, weights, arrays, cuts, tile):
    rows, heads = arrays[0].shape
    spans = [(a // tile, b // tile) for a, b in cuts]

    def piece_spec(first, end):
        return pl.BlockSpec((tile, heads), lambda i: (jnp.clip(i - first, 0, end - first - 1), 0))

    block = pl.BlockSpec((tile, heads), lambda i: (i, 0))
    return pl.pallas_call(
        functools.partial(body, spans),
        grid=(rows // tile,),
        in_specs=[pl.BlockSpec(memory_space=pltpu.SMEM)] + [block] * len(arrays),
        out_specs=[block] + [piece_spec(*span) for span in spans],
        out_shape=[jax.ShapeDtypeStruct((rows, heads), jnp.float32)]
        + [jax.ShapeDtypeStruct((b - a, heads), jnp.float32) for a, b in cuts],
        compiler_params=pltpu.CompilerParams(
            dimension_semantics=("arbitrary",), vmem_limit_bytes=8 * 2**20
        ),
        cost_estimate=pl.CostEstimate(
            flops=8 * rows * heads, bytes_accessed=28 * rows * heads, transcendentals=0
        ),
    )(weights, *arrays)


def combine(mix_weights, own, from_row, from_col):
    return mix_weights[0] * own + mix_weights[1] * from_row + mix_weights[2] * from_col


def on_device(value_proj, token_pool, target_pool, batch_ids, frozen_out, numerators):
    counts = numerators.astype(jnp.float32)
    mix_weights = counts / jnp.sum(counts)
    current = value_proj[0, 0]
    width = current.shape[0]
    tile = width // 8
    cuts = [(0, width // 2), (width // 2, width - tile), (width - tile, width)]

    def gradient_at(field, which):
        return local_gradient(
            which, field, token_pool[0, 0], target_pool[0, 0], batch_ids[0, 0], frozen_out
        )

    def neighbours(field):
        from_col = shifted(field, "col", 1)
        return shifted(field, "row", 1), from_col

    around_current = neighbours(current)
    grad_old = gradient_at(current, 0)
    tracker = grad_old
    for which in range(1, ITERS + 1):
        final = which == ITERS
        if which == 1:
            around_tracker = neighbours(tracker)
        current = combine(mix_weights, current, *around_current) - step_rate * tracker
        if not final:
            around_current = neighbours(current)
        grad_new = gradient_at(current, which)
        if not final:
            arrays = (tracker, *around_tracker, grad_new, grad_old)
            ends = cuts if which == ITERS - 1 else []
            tracker, *blocks = sweep(track_body, mix_weights, arrays, ends, tile)
            if which < ITERS - 1:
                around_tracker = neighbours(tracker)
            else:
                pieces = [shifted(b, "col", 1) for b in blocks]
                track_row = shifted(tracker, "row", 1)
            grad_old = grad_new

    arrays = (tracker, track_row, grad_new, grad_old)
    result, last = sweep(near_body, mix_weights, arrays, cuts[-1:], tile)
    for (start, _), piece in zip(cuts[:-1], pieces):
        result = add_piece(mix_weights[2:], result, piece, start)
    result = add_tail(mix_weights[2:], result, last, pieces[-1], cuts[-1][0])
    return (current[None, None], result[None, None])


def solution(mesh):
    whole = P("row", "col", None, None)
    return jax.shard_map(
        on_device,
        mesh=mesh,
        in_specs=(whole, whole, whole, whole, P(), P()),
        out_specs=(whole, whole),
        check_vma=False,
    )
```

profile of v0, /device:TPU:0, one launch (start us, length us, event | category | flops | bytes accessed | tf_op | source)
XLA Modules:
  0.0 195.7 jit_solution(9997629720529315829)
XLA Ops:
  0.6 3.1 %collective-permute-start.1 = (f32[1024,512]{1,0:T(8,128)}, f32[1024,512]{1,0:T(8,128)S(1)}, u32[]{:S(2)}, u32[]{:S(2)}) collective-permute-start(f32[1024,512]{1,0:T(8,128)} %bitcast.12), channel_id=1, source_target_pairs={{3,0},{0,1},{1,2},{2,3},{7,4},{4,5},{5,6},{6,7},{11,8},{8,9},{9,10... | collective-permute-start | bytes 6291464 | tf_op jit(solution)/shard_map/ppermute | solution.py:19
  3.7 0.7 copy.13
  4.5 1.6 copy-done
  6.1 1.9 copy-done.2
  8.0 1.9 copy-done.4
  9.8 1.2 copy-done.6
  11.1 8.9 %shard_map.77.own_ref.old_ref = f32[1024,512]{1,0:T(8,128)S(1)} custom-call(s32[3,1536]{1,0:T(4,128)S(1)} %bitcast.16, f32[1024,512]{1,0:T(8,128)S(1)} %bitcast.14, bf16[1536,1024]{1,0:T(8,128)(2,1)S(1)} %bitcast.19, bf16[1536,1024]{1,0:T(8,128)(2,1)S(1)} %bitcast.22, bf16[512,1024]{1,0:T(8,128)(2,1)S(1)} %copy-done.6), custom_call_target="tpu_custom_call" | custom-call | flops 6442450944 | bytes 12582912 | tf_op jit(solution)/shard_map/pallas_call | solution.py:69
  20.0 1.6 collective-permute-start.5
  21.6 1.3 collective-permute-start.4
  22.9 0.6 convert_reduce_fusion
  23.5 0.6 convert_divide_fusion.w_ref
  24.2 0.7 fusion
  24.9 27.6 %collective-permute-done.1 = f32[1024,512]{1,0:T(8,128)S(1)} collective-permute-done((f32[1024,512]{1,0:T(8,128)}, f32[1024,512]{1,0:T(8,128)S(1)}, u32[]{:S(2)}, u32[]{:S(2)}) %collective-permute-start.1) | collective-permute-done | bytes 2097184 | tf_op jit(solution)/shard_map/ppermute | solution.py:19
  52.5 3.8 %multiply_subtract_fusion.1.x_ref = f32[1024,512]{1,0:T(8,128)S(1)} fusion(f32[1024,512]{1,0:T(8,128)S(1)} %shard_map.77.own_ref.old_ref, f32[1024,512]{1,0:T(8,128)S(1)} %collective-permute-done.1, f32[1024,512]{1,0:T(8,128)S(1)} %collective-permute-done, f32[]{:T(128)} %bitcast.3, f32[]{:T(128)} %bitcast.2, f32[]{:T(128)} %bitcast, ...), kind=kLoop, calls=%fused_computation.1 | loop fusion | flops 3670016 | bytes 10485772 | tf_op jit(solution)/shard_map/sub | solution.py:222
  56.3 0.1 collective-permute-start.3
  56.4 0.1 collective-permute-start.2
  56.5 8.9 %shard_map.78.new_ref.old_ref = f32[1024,512]{1,0:T(8,128)S(1)} custom-call(s32[3,1536]{1,0:T(4,128)S(1)} %bitcast.17, f32[1024,512]{1,0:T(8,128)S(1)} %multiply_subtract_fusion.1.x_ref, bf16[1536,1024]{1,0:T(8,128)(2,1)S(1)} %bitcast.20, bf16[1536,1024]{1,0:T(8,128)(2,1)S(1)} %bitcast.23, bf16[512,1024]{1,0:T(8,128)(2,1)S(1)} %copy-done.7), custom_call_target="tpu_custom_call" | custom-call | flops 6442450944 | bytes 12582912 | tf_op jit(solution)/shard_map/pallas_call | solution.py:69
  65.4 32.0 %collective-permute-done.5.col_ref = f32[1024,512]{1,0:T(8,128)S(1)} collective-permute-done((f32[1024,512]{1,0:T(8,128)S(1)}, f32[1024,512]{1,0:T(8,128)S(1)}, u32[]{:S(2)}, u32[]{:S(2)}) %collective-permute-start.5) | collective-permute-done | bytes 2097184 | tf_op jit(solution)/shard_map/ppermute | solution.py:19
  97.4 1.4 shard_map.79
  98.8 0.1 collective-permute-start.6
  98.9 0.1 collective-permute-start.9
  99.0 1.6 collective-permute-start.8
  100.5 41.8 %collective-permute-done.3 = f32[1024,512]{1,0:T(8,128)S(1)} collective-permute-done((f32[1024,512]{1,0:T(8,128)S(1)}, f32[1024,512]{1,0:T(8,128)S(1)}, u32[]{:S(2)}, u32[]{:S(2)}) %collective-permute-start.3) | collective-permute-done | bytes 2097184 | tf_op jit(solution)/shard_map/ppermute | solution.py:19
  142.3 0.0 collective-permute-start.7
  142.3 3.0 %multiply_subtract_fusion.x_ref = f32[1024,512]{1,0:T(8,128)S(1)} fusion(f32[1024,512]{1,0:T(8,128)S(1)} %get-tuple-element.8.own_ref, f32[1024,512]{1,0:T(8,128)S(1)} %collective-permute-done.3, f32[1024,512]{1,0:T(8,128)S(1)} %collective-permute-done.2, f32[1024,512]{1,0:T(8,128)S(1)} %multiply_subtract_fusion.1.x_ref, f32[]{:T(128)} %bitcast.3, f32[]{:T(128)} %bitcast.2, ...), kind=kLoop, calls=%fused_computation | loop fusion | flops 3670016 | bytes 10485772 | tf_op jit(solution)/shard_map/sub | solution.py:222
  145.4 0.0 copy-start.1
  145.4 8.9 %shard_map.80.new_ref = f32[1024,512]{1,0:T(8,128)S(1)} custom-call(s32[3,1536]{1,0:T(4,128)S(1)} %bitcast.18, f32[1024,512]{1,0:T(8,128)S(1)} %multiply_subtract_fusion.x_ref, bf16[1536,1024]{1,0:T(8,128)(2,1)S(1)} %bitcast.21, bf16[1536,1024]{1,0:T(8,128)(2,1)S(1)} %bitcast.24, bf16[512,1024]{1,0:T(8,128)(2,1)S(1)} %copy-done.7), custom_call_target="tpu_custom_call" | custom-call | flops 6442450944 | bytes 12582912 | tf_op jit(solution)/shard_map/pallas_call | solution.py:69
  154.3 3.7 %shard_map.81 = (f32[1024,512]{1,0:T(8,128)}, f32[128,512]{1,0:T(8,128)S(1)}) custom-call(f32[3]{0:T(128)S(1)} %convert_divide_fusion.w_ref, f32[1024,512]{1,0:T(8,128)S(1)} %get-tuple-element.8.own_ref, f32[1024,512]{1,0:T(8,128)S(1)} %collective-permute-done.6.row_ref, f32[1024,512]{1,0:T(8,128)S(1)} %shard_map.80.new_ref, ...), custom_call_target="tpu_custom_call" | custom-call | flops 4194304 | bytes 14680064 | tf_op jit(solution)/shard_map/pallas_call | solution.py:178
  158.1 28.4 %collective-permute-done.7.piece_ref = f32[512,512]{1,0:T(8,128)S(1)} collective-permute-done((f32[512,512]{1,0:T(8,128)S(1)}, f32[512,512]{1,0:T(8,128)S(1)}, u32[]{:S(2)}, u32[]{:S(2)}) %collective-permute-start.7) | collective-permute-done | bytes 1048608 | tf_op jit(solution)/shard_map/ppermute | solution.py:19
  186.4 4.1 %add_piece.2.rest_ref = f32[1024,512]{1,0:T(8,128)} custom-call(f32[1]{0:T(128)} %get-tuple-element.15.weight_ref, f32[1024,512]{1,0:T(8,128)} %get-tuple-element.9.rest_ref, f32[512,512]{1,0:T(8,128)S(1)} %collective-permute-done.7.piece_ref), custom_call_target="tpu_custom_call", output_to_operand_aliasing={{}: (1, {})} | custom-call | flops 524288 | bytes 3145728 | tf_op jit(solution)/shard_map/add_piece/pallas_call | solution.py:99
  190.5 3.6 %add_piece.3.filled_ref = f32[1024,512]{1,0:T(8,128)} custom-call(f32[1]{0:T(128)} %get-tuple-element.15.weight_ref, f32[1024,512]{1,0:T(8,128)} %add_piece.2.rest_ref, f32[384,512]{1,0:T(8,128)S(1)} %collective-permute-done.8.piece_ref), custom_call_target="tpu_custom_call", output_to_operand_aliasing={{}: (1, {})} | custom-call | flops 393216 | bytes 2359296 | tf_op jit(solution)/shard_map/add_piece/pallas_call | solution.py:99
  194.1 1.4 add_tail.1
  (20 shorter events, 0.0 us)
Async XLA Ops:
  0.6 51.8 %collective-permute-start.1 = (f32[1024,512]{1,0:T(8,128)}, f32[1024,512]{1,0:T(8,128)S(1)}, u32[]{:S(2)}, u32[]{:S(2)}) collective-permute-start(f32[1024,512]{1,0:T(8,128)} %bitcast.12), channel_id=1, source_target_pairs={{3,0},{0,1},{1,2},{2,3},{7,4},{4,5},{5,6},{6,7},{11,8},{8,9},{9,10... | collective-permute-start | bytes 6291464 | tf_op jit(solution)/shard_map/ppermute | solution.py:19
  3.7 48.7 %collective-permute-start = (f32[1024,512]{1,0:T(8,128)}, f32[1024,512]{1,0:T(8,128)S(1)}, u32[]{:S(2)}, u32[]{:S(2)}) collective-permute-start(f32[1024,512]{1,0:T(8,128)} %bitcast.13), channel_id=1, source_target_pairs={{28,0},{0,4},{4,8},{8,12},{12,16},{16,20},{20,24},{24,28},{29,1},{... | collective-permute-start | bytes 6291464 | tf_op jit(solution)/shard_map/ppermute | solution.py:19
  4.5 1.6 copy-start
  6.1 1.9 copy-start.2
  7.9 1.9 copy-start.4
  9.8 1.2 copy-start.6
  11.1 11.9 %copy-start.8 = (s32[3]{0:T(128)S(1)}, s32[3]{0:T(128)}, u32[]{:S(2)}) copy-start(s32[3]{0:T(128)} %param.11) | copy-start | bytes 40
  20.0 77.4 %collective-permute-start.5 = (f32[1024,512]{1,0:T(8,128)S(1)}, f32[1024,512]{1,0:T(8,128)S(1)}, u32[]{:S(2)}, u32[]{:S(2)}) collective-permute-start(f32[1024,512]{1,0:T(8,128)S(1)} %shard_map.77.own_ref.old_ref), channel_id=1, source_target_pairs={{3,0},{0,1},{1,2},{2,3},{7,4},{4,5},{5,6},{6,7},{11,8},{8,9},{9,10... | collective-permute-start | bytes 6291464 | tf_op jit(solution)/shard_map/ppermute | solution.py:19
  21.6 75.8 %collective-permute-start.4 = (f32[1024,512]{1,0:T(8,128)S(1)}, f32[1024,512]{1,0:T(8,128)S(1)}, u32[]{:S(2)}, u32[]{:S(2)}) collective-permute-start(f32[1024,512]{1,0:T(8,128)S(1)} %shard_map.77.own_ref.old_ref), channel_id=1, source_target_pairs={{28,0},{0,4},{4,8},{8,12},{12,16},{16,20},{20,24},{24,28},{29,1},{... | collective-permute-start | bytes 6291464 | tf_op jit(solution)/shard_map/ppermute | solution.py:19
  52.5 4.0 %copy-start.3 = (bf16[1,1,1536,1024]{3,2,1,0:T(8,128)(2,1)S(1)}, bf16[1,1,1536,1024]{3,2,1,0:T(8,128)(2,1)}, u32[]{:S(2)}) copy-start(bf16[1,1,1536,1024]{3,2,1,0:T(8,128)(2,1)} %param.7) | copy-start | bytes 9437188
  52.5 4.0 %copy-start.5 = (bf16[1,1,1536,1024]{3,2,1,0:T(8,128)(2,1)S(1)}, bf16[1,1,1536,1024]{3,2,1,0:T(8,128)(2,1)}, u32[]{:S(2)}) copy-start(bf16[1,1,1536,1024]{3,2,1,0:T(8,128)(2,1)} %param.8) | copy-start | bytes 9437188
  52.5 4.0 %copy-start.7 = (bf16[512,1024]{1,0:T(8,128)(2,1)S(1)}, bf16[512,1024]{1,0:T(8,128)(2,1)}, u32[]{:S(2)}) copy-start(bf16[512,1024]{1,0:T(8,128)(2,1)} %out_ref.5) | copy-start | bytes 3145732
  56.3 86.0 %collective-permute-start.3 = (f32[1024,512]{1,0:T(8,128)S(1)}, f32[1024,512]{1,0:T(8,128)S(1)}, u32[]{:S(2)}, u32[]{:S(2)}) collective-permute-start(f32[1024,512]{1,0:T(8,128)S(1)} %multiply_subtract_fusion.1.x_ref), channel_id=1, source_target_pairs={{3,0},{0,1},{1,2},{2,3},{7,4},{4,5},{5,6},{6,7},{11,8},{8,9},{9,10... | collective-permute-start | bytes 6291464 | tf_op jit(solution)/shard_map/ppermute | solution.py:19
  56.4 86.0 %collective-permute-start.2 = (f32[1024,512]{1,0:T(8,128)S(1)}, f32[1024,512]{1,0:T(8,128)S(1)}, u32[]{:S(2)}, u32[]{:S(2)}) collective-permute-start(f32[1024,512]{1,0:T(8,128)S(1)} %multiply_subtract_fusion.1.x_ref), channel_id=1, source_target_pairs={{28,0},{0,4},{4,8},{8,12},{12,16},{16,20},{20,24},{24,28},{29,1},{... | collective-permute-start | bytes 6291464 | tf_op jit(solution)/shard_map/ppermute | solution.py:19
  98.8 55.5 %collective-permute-start.6 = (f32[1024,512]{1,0:T(8,128)S(1)}, f32[1024,512]{1,0:T(8,128)S(1)}, u32[]{:S(2)}, u32[]{:S(2)}) collective-permute-start(f32[1024,512]{1,0:T(8,128)S(1)} %get-tuple-element.8.own_ref), channel_id=1, source_target_pairs={{28,0},{0,4},{4,8},{8,12},{12,16},{16,20},{20,24},{24,28},{29,1},{... | collective-permute-start | bytes 6291464 | tf_op jit(solution)/shard_map/ppermute | solution.py:19
  98.9 95.2 %collective-permute-start.9 = (f32[128,512]{1,0:T(8,128)S(1)}, f32[128,512]{1,0:T(8,128)S(1)}, u32[]{:S(2)}, u32[]{:S(2)}) collective-permute-start(f32[128,512]{1,0:T(8,128)S(1)} %get-tuple-element.13), channel_id=1, source_target_pairs={{3,0},{0,1},{1,2},{2,3},{7,4},{4,5},{5,6},{6,7},{11,8},{8,9},{9,10... | collective-permute-start | bytes 786440 | tf_op jit(solution)/shard_map/ppermute | solution.py:19
  99.0 91.5 %collective-permute-start.8 = (f32[384,512]{1,0:T(8,128)S(1)}, f32[384,512]{1,0:T(8,128)S(1)}, u32[]{:S(2)}, u32[]{:S(2)}) collective-permute-start(f32[384,512]{1,0:T(8,128)S(1)} %get-tuple-element.11), channel_id=1, source_target_pairs={{3,0},{0,1},{1,2},{2,3},{7,4},{4,5},{5,6},{6,7},{11,8},{8,9},{9,10... | collective-permute-start | bytes 2359304 | tf_op jit(solution)/shard_map/ppermute | solution.py:19
  142.3 44.1 %collective-permute-start.7 = (f32[512,512]{1,0:T(8,128)S(1)}, f32[512,512]{1,0:T(8,128)S(1)}, u32[]{:S(2)}, u32[]{:S(2)}) collective-permute-start(f32[512,512]{1,0:T(8,128)S(1)} %get-tuple-element.10), channel_id=1, source_target_pairs={{3,0},{0,1},{1,2},{2,3},{7,4},{4,5},{5,6},{6,7},{11,8},{8,9},{9,10... | collective-permute-start | bytes 3145736 | tf_op jit(solution)/shard_map/ppermute | solution.py:19
  145.4 8.9 %copy-start.1 = (f32[1024,512]{1,0:T(8,128)}, f32[1024,512]{1,0:T(8,128)S(1)}, u32[]{:S(2)}) copy-start(f32[1024,512]{1,0:T(8,128)S(1)} %multiply_subtract_fusion.x_ref) | copy-start | bytes 6291460
where the time goes:
time: 196 us
  waiting for transfers between devices  130 us (66%)
  Pallas kernels  41 us (21%)
  other arithmetic  8.12 us (4%)
  local copies, waits for them, and re-layouts  8 us (4%)
  starting transfers between devices  7.83 us (4%)
    ppermute x10, waiting for transfers between devices, shifted(): return lax.ppermute(block, axis, route)  130 us
    pallas_call x3, Pallas kernels, local_gradient(): pl.pallas_call(functools.partial(gradient_body, which, tile, width ** (-0...  26.8 us
    ppermute x10, starting transfers between devices, shifted(): return lax.ppermute(block, axis, route)  7.83 us
    pallas_call x2, Pallas kernels, add_piece(): pl.pallas_call(add_body, grid=(rows // tile,), in_specs=[pl.BlockSpec(mem...  7.65 us
    unnamed x19, local copies, waits for them, and re-layouts  7.34 us
    sub x2, other arithmetic, on_device(): combine(mix_weights, current, *around_current) - step_rate * tracker  6.87 us
    pallas_call x2, Pallas kernels, sweep(): pl.pallas_call(functools.partial(body, spans), grid=(rows // tile,), in_s...  5.16 us
  transfers between devices with their start and end apart: 10, of which 4 were waited for; matrix products, arithmetic and copies ran while one was open for 5% of the time, Pallas kernels for 20%

commit v1 on v0

--- a/solution.py
+++ b/solution.py
@@ -88,11 +88,11 @@
     )(ids, current, tokens, targets, frozen_out)
 
 
-def add_body(weight_ref, rest_ref, piece_ref, out_ref):
-    out_ref[...] = rest_ref[...] + weight_ref[0] * piece_ref[...]
-
-
-def add_piece(weight, rest, piece, start):
+def add_body(rest_ref, piece_ref, out_ref):
+    out_ref[...] = rest_ref[...] + piece_ref[...]
+
+
+def add_piece(rest, piece, start):
     rows, heads = piece.shape
     tile = tile_of(rows, 128)
     first = start // tile
@@ -100,34 +100,32 @@
         add_body,
         grid=(rows // tile,),
         in_specs=[
-            pl.BlockSpec(memory_space=pltpu.SMEM),
             pl.BlockSpec((tile, heads), lambda i: (i + first, 0)),
             pl.BlockSpec((tile, heads), lambda i: (i, 0)),
         ],
         out_specs=pl.BlockSpec((tile, heads), lambda i: (i + first, 0)),
         out_shape=jax.ShapeDtypeStruct(rest.shape, rest.dtype),
-        input_output_aliases={1: 0},
+        input_output_aliases={0: 0},
         compiler_params=pltpu.CompilerParams(vmem_limit_bytes=4 * 2**20),
         cost_estimate=pl.CostEstimate(
             flops=2 * rows * heads, bytes_accessed=12 * rows * heads, transcendentals=0
         ),
         name="add_piece",
-    )(weight, rest, piece)
-
-
-def tail_body(start, weight_ref, filled_ref, rest_ref, piece_ref, out_ref, sum_ref, sem):
-    sum_ref[...] = rest_ref[...] + weight_ref[0] * piece_ref[...]
+    )(rest, piece)
+
+
+def tail_body(start, filled_ref, rest_ref, piece_ref, out_ref, sum_ref, sem):
+    sum_ref[...] = rest_ref[...] + piece_ref[...]
     copy = pltpu.make_async_copy(sum_ref, out_ref.at[pl.ds(start, sum_ref.shape[0])], sem)
     copy.start()
     copy.wait()
 
 
-def add_tail(weight, filled, rest, piece, start):
+def add_tail(filled, rest, piece, start):
     rows, heads = piece.shape
     return pl.pallas_call(
         functools.partial(tail_body, start),
         in_specs=[
-            pl.BlockSpec(memory_space=pltpu.SMEM),
             pl.BlockSpec(memory_space=pl.ANY),
             pl.BlockSpec(memory_space=pltpu.VMEM),
             pl.BlockSpec(memory_space=pltpu.VMEM),
@@ -135,13 +133,13 @@
         out_specs=pl.BlockSpec(memory_space=pl.ANY),
         out_shape=jax.ShapeDtypeStruct(filled.shape, filled.dtype),
         scratch_shapes=[pltpu.VMEM(piece.shape, piece.dtype), pltpu.SemaphoreType.DMA],
-        input_output_aliases={1: 0},
+        input_output_aliases={0: 0},
         compiler_params=pltpu.CompilerParams(vmem_limit_bytes=4 * 2**20),
         cost_estimate=pl.CostEstimate(
             flops=2 * rows * heads, bytes_accessed=12 * rows * heads, transcendentals=0
         ),
         name="add_tail",
-    )(weight, filled, rest, piece)
+    )(filled, rest, piece)
 
 
 def track_body(spans, w_ref, own_ref, row_ref, col_ref, new_ref, old_ref, all_ref, *piece_refs):
@@ -153,7 +151,7 @@
 
         @pl.when((step >= first) & (step < end))
         def _():
-            piece_ref[...] = tracker
+            piece_ref[...] = w_ref[2] * tracker
 
 
 def near_body(spans, w_ref, own_ref, row_ref, new_ref, old_ref, all_ref, *piece_refs):
@@ -237,8 +235,8 @@
     arrays = (tracker, track_row, grad_new, grad_old)
     result, last = sweep(near_body, mix_weights, arrays, cuts[-1:], tile)
     for (start, _), piece in zip(cuts[:-1], pieces):
-        result = add_piece(mix_weights[2:], result, piece, start)
-    result = add_tail(mix_weights[2:], result, last, pieces[-1], cuts[-1][0])
+        result = add_piece(result, piece, start)
+    result = add_tail(result, last, pieces[-1], cuts[-1][0])
     return (current[None, None], result[None, None])
 
 

time: 196 us -> 194 us (0.990)
  Pallas kernels: 41 us -> 39 us
where the time goes in v1:
time: 194 us
  waiting for transfers between devices  130 us (67%)
  Pallas kernels  39 us (20%)
  other arithmetic  8.12 us (4%)
  local copies, waits for them, and re-layouts  8 us (4%)
  starting transfers between devices  7.83 us (4%)
    ppermute x10, waiting for transfers between devices, shifted(): return lax.ppermute(block, axis, route)  130 us
    pallas_call x3, Pallas kernels, local_gradient(): pl.pallas_call(functools.partial(gradient_body, which, tile, width ** (-0...  26.8 us
    ppermute x10, starting transfers between devices, shifted(): return lax.ppermute(block, axis, route)  7.83 us
    unnamed x19, local copies, waits for them, and re-layouts  7.34 us
    sub x2, other arithmetic, on_device(): combine(mix_weights, current, *around_current) - step_rate * tracker  6.87 us
    pallas_call x2, Pallas kernels, add_piece(): pl.pallas_call(add_body, grid=(rows // tile,), in_specs=[pl.BlockSpec((ti...  6.24 us
    pallas_call x2, Pallas kernels, sweep(): pl.pallas_call(functools.partial(body, spans), grid=(rows // tile,), in_s...  5.23 us
  transfers between devices with their start and end apart: 10, of which 4 were waited for; matrix products, arithmetic and copies ran while one was open for 5% of the time, Pallas kernels for 20%

profile of v1, /device:TPU:0, one launch (start us, length us, event | category | flops | bytes accessed | tf_op | source)
XLA Modules:
  0.0 193.6 jit_solution(8427127843099012331)
XLA Ops:
  0.6 3.1 %collective-permute-start.1 = (f32[1024,512]{1,0:T(8,128)}, f32[1024,512]{1,0:T(8,128)S(1)}, u32[]{:S(2)}, u32[]{:S(2)}) collective-permute-start(f32[1024,512]{1,0:T(8,128)} %bitcast.12), channel_id=1, source_target_pairs={{3,0},{0,1},{1,2},{2,3},{7,4},{4,5},{5,6},{6,7},{11,8},{8,9},{9,10... | collective-permute-start | bytes 6291464 | tf_op jit(solution)/shard_map/ppermute | solution.py:19
  3.7 0.7 copy.13
  4.5 1.6 copy-done
  6.1 1.9 copy-done.2
  8.0 1.9 copy-done.4
  9.8 1.2 copy-done.6
  11.1 8.9 %shard_map.77.own_ref.old_ref = f32[1024,512]{1,0:T(8,128)S(1)} custom-call(s32[3,1536]{1,0:T(4,128)S(1)} %bitcast.16, f32[1024,512]{1,0:T(8,128)S(1)} %bitcast.14, bf16[1536,1024]{1,0:T(8,128)(2,1)S(1)} %bitcast.19, bf16[1536,1024]{1,0:T(8,128)(2,1)S(1)} %bitcast.22, bf16[512,1024]{1,0:T(8,128)(2,1)S(1)} %copy-done.6), custom_call_target="tpu_custom_call" | custom-call | flops 6442450944 | bytes 12582912 | tf_op jit(solution)/shard_map/pallas_call | solution.py:69
  20.0 1.6 collective-permute-start.5
  21.6 1.3 collective-permute-start.4
  22.9 0.6 convert_reduce_fusion
  23.5 0.6 convert_divide_fusion.w_ref
  24.2 0.7 fusion
  24.9 27.6 %collective-permute-done.1 = f32[1024,512]{1,0:T(8,128)S(1)} collective-permute-done((f32[1024,512]{1,0:T(8,128)}, f32[1024,512]{1,0:T(8,128)S(1)}, u32[]{:S(2)}, u32[]{:S(2)}) %collective-permute-start.1) | collective-permute-done | bytes 2097184 | tf_op jit(solution)/shard_map/ppermute | solution.py:19
  52.5 3.8 %multiply_subtract_fusion.1.x_ref = f32[1024,512]{1,0:T(8,128)S(1)} fusion(f32[1024,512]{1,0:T(8,128)S(1)} %shard_map.77.own_ref.old_ref, f32[1024,512]{1,0:T(8,128)S(1)} %collective-permute-done.1, f32[1024,512]{1,0:T(8,128)S(1)} %collective-permute-done, f32[]{:T(128)} %bitcast.3, f32[]{:T(128)} %bitcast.2, f32[]{:T(128)} %bitcast, ...), kind=kLoop, calls=%fused_computation.1 | loop fusion | flops 3670016 | bytes 10485772 | tf_op jit(solution)/shard_map/sub | solution.py:220
  56.3 0.1 collective-permute-start.3
  56.4 0.1 collective-permute-start.2
  56.5 8.9 %shard_map.78.new_ref.old_ref = f32[1024,512]{1,0:T(8,128)S(1)} custom-call(s32[3,1536]{1,0:T(4,128)S(1)} %bitcast.17, f32[1024,512]{1,0:T(8,128)S(1)} %multiply_subtract_fusion.1.x_ref, bf16[1536,1024]{1,0:T(8,128)(2,1)S(1)} %bitcast.20, bf16[1536,1024]{1,0:T(8,128)(2,1)S(1)} %bitcast.23, bf16[512,1024]{1,0:T(8,128)(2,1)S(1)} %copy-done.7), custom_call_target="tpu_custom_call" | custom-call | flops 6442450944 | bytes 12582912 | tf_op jit(solution)/shard_map/pallas_call | solution.py:69
  65.4 32.0 %collective-permute-done.5.col_ref = f32[1024,512]{1,0:T(8,128)S(1)} collective-permute-done((f32[1024,512]{1,0:T(8,128)S(1)}, f32[1024,512]{1,0:T(8,128)S(1)}, u32[]{:S(2)}, u32[]{:S(2)}) %collective-permute-start.5) | collective-permute-done | bytes 2097184 | tf_op jit(solution)/shard_map/ppermute | solution.py:19
  97.4 1.5 shard_map.79
  98.9 0.1 collective-permute-start.6
  99.0 0.1 collective-permute-start.9
  99.0 1.6 collective-permute-start.8
  100.6 41.7 %collective-permute-done.3 = f32[1024,512]{1,0:T(8,128)S(1)} collective-permute-done((f32[1024,512]{1,0:T(8,128)S(1)}, f32[1024,512]{1,0:T(8,128)S(1)}, u32[]{:S(2)}, u32[]{:S(2)}) %collective-permute-start.3) | collective-permute-done | bytes 2097184 | tf_op jit(solution)/shard_map/ppermute | solution.py:19
  142.3 0.0 collective-permute-start.7
  142.3 3.0 %multiply_subtract_fusion.x_ref = f32[1024,512]{1,0:T(8,128)S(1)} fusion(f32[1024,512]{1,0:T(8,128)S(1)} %get-tuple-element.8.own_ref, f32[1024,512]{1,0:T(8,128)S(1)} %collective-permute-done.3, f32[1024,512]{1,0:T(8,128)S(1)} %collective-permute-done.2, f32[1024,512]{1,0:T(8,128)S(1)} %multiply_subtract_fusion.1.x_ref, f32[]{:T(128)} %bitcast.3, f32[]{:T(128)} %bitcast.2, ...), kind=kLoop, calls=%fused_computation | loop fusion | flops 3670016 | bytes 10485772 | tf_op jit(solution)/shard_map/sub | solution.py:220
  145.4 0.0 copy-start.1
  145.4 8.9 %shard_map.80.new_ref = f32[1024,512]{1,0:T(8,128)S(1)} custom-call(s32[3,1536]{1,0:T(4,128)S(1)} %bitcast.18, f32[1024,512]{1,0:T(8,128)S(1)} %multiply_subtract_fusion.x_ref, bf16[1536,1024]{1,0:T(8,128)(2,1)S(1)} %bitcast.21, bf16[1536,1024]{1,0:T(8,128)(2,1)S(1)} %bitcast.24, bf16[512,1024]{1,0:T(8,128)(2,1)S(1)} %copy-done.7), custom_call_target="tpu_custom_call" | custom-call | flops 6442450944 | bytes 12582912 | tf_op jit(solution)/shard_map/pallas_call | solution.py:69
  154.3 3.7 %shard_map.81 = (f32[1024,512]{1,0:T(8,128)}, f32[128,512]{1,0:T(8,128)S(1)}) custom-call(f32[3]{0:T(128)S(1)} %convert_divide_fusion.w_ref, f32[1024,512]{1,0:T(8,128)S(1)} %get-tuple-element.8.own_ref, f32[1024,512]{1,0:T(8,128)S(1)} %collective-permute-done.6.row_ref, f32[1024,512]{1,0:T(8,128)S(1)} %shard_map.80.new_ref, ...), custom_call_target="tpu_custom_call" | custom-call | flops 4194304 | bytes 14680064 | tf_op jit(solution)/shard_map/pallas_call | solution.py:176
  158.1 28.4 %collective-permute-done.7.piece_ref = f32[512,512]{1,0:T(8,128)S(1)} collective-permute-done((f32[512,512]{1,0:T(8,128)S(1)}, f32[512,512]{1,0:T(8,128)S(1)}, u32[]{:S(2)}, u32[]{:S(2)}) %collective-permute-start.7) | collective-permute-done | bytes 1048608 | tf_op jit(solution)/shard_map/ppermute | solution.py:19
  186.4 3.4 %add_piece.2.rest_ref = f32[1024,512]{1,0:T(8,128)} custom-call(f32[1024,512]{1,0:T(8,128)} %get-tuple-element.9.rest_ref, f32[512,512]{1,0:T(8,128)S(1)} %collective-permute-done.7.piece_ref), custom_call_target="tpu_custom_call", output_to_operand_aliasing={{}: (0, {})} | custom-call | flops 524288 | bytes 3145728 | tf_op jit(solution)/shard_map/add_piece/pallas_call | solution.py:99
  189.8 2.9 %add_piece.3.filled_ref = f32[1024,512]{1,0:T(8,128)} custom-call(f32[1024,512]{1,0:T(8,128)} %add_piece.2.rest_ref, f32[384,512]{1,0:T(8,128)S(1)} %collective-permute-done.8.piece_ref), custom_call_target="tpu_custom_call", output_to_operand_aliasing={{}: (0, {})} | custom-call | flops 393216 | bytes 2359296 | tf_op jit(solution)/shard_map/add_piece/pallas_call | solution.py:99
  192.7 0.7 add_tail.1
  (20 shorter events, 0.0 us)
Async XLA Ops:
  0.6 51.8 %collective-permute-start.1 = (f32[1024,512]{1,0:T(8,128)}, f32[1024,512]{1,0:T(8,128)S(1)}, u32[]{:S(2)}, u32[]{:S(2)}) collective-permute-start(f32[1024,512]{1,0:T(8,128)} %bitcast.12), channel_id=1, source_target_pairs={{3,0},{0,1},{1,2},{2,3},{7,4},{4,5},{5,6},{6,7},{11,8},{8,9},{9,10... | collective-permute-start | bytes 6291464 | tf_op jit(solution)/shard_map/ppermute | solution.py:19
  3.7 48.7 %collective-permute-start = (f32[1024,512]{1,0:T(8,128)}, f32[1024,512]{1,0:T(8,128)S(1)}, u32[]{:S(2)}, u32[]{:S(2)}) collective-permute-start(f32[1024,512]{1,0:T(8,128)} %bitcast.13), channel_id=1, source_target_pairs={{28,0},{0,4},{4,8},{8,12},{12,16},{16,20},{20,24},{24,28},{29,1},{... | collective-permute-start | bytes 6291464 | tf_op jit(solution)/shard_map/ppermute | solution.py:19
  4.5 1.6 copy-start
  6.1 1.9 copy-start.2
  7.9 1.9 copy-start.4
  9.8 1.2 copy-start.6
  11.1 11.9 %copy-start.8 = (s32[3]{0:T(128)S(1)}, s32[3]{0:T(128)}, u32[]{:S(2)}) copy-start(s32[3]{0:T(128)} %param.11) | copy-start | bytes 40
  20.0 77.4 %collective-permute-start.5 = (f32[1024,512]{1,0:T(8,128)S(1)}, f32[1024,512]{1,0:T(8,128)S(1)}, u32[]{:S(2)}, u32[]{:S(2)}) collective-permute-start(f32[1024,512]{1,0:T(8,128)S(1)} %shard_map.77.own_ref.old_ref), channel_id=1, source_target_pairs={{3,0},{0,1},{1,2},{2,3},{7,4},{4,5},{5,6},{6,7},{11,8},{8,9},{9,10... | collective-permute-start | bytes 6291464 | tf_op jit(solution)/shard_map/ppermute | solution.py:19
  21.6 75.8 %collective-permute-start.4 = (f32[1024,512]{1,0:T(8,128)S(1)}, f32[1024,512]{1,0:T(8,128)S(1)}, u32[]{:S(2)}, u32[]{:S(2)}) collective-permute-start(f32[1024,512]{1,0:T(8,128)S(1)} %shard_map.77.own_ref.old_ref), channel_id=1, source_target_pairs={{28,0},{0,4},{4,8},{8,12},{12,16},{16,20},{20,24},{24,28},{29,1},{... | collective-permute-start | bytes 6291464 | tf_op jit(solution)/shard_map/ppermute | solution.py:19
  52.5 4.0 %copy-start.3 = (bf16[1,1,1536,1024]{3,2,1,0:T(8,128)(2,1)S(1)}, bf16[1,1,1536,1024]{3,2,1,0:T(8,128)(2,1)}, u32[]{:S(2)}) copy-start(bf16[1,1,1536,1024]{3,2,1,0:T(8,128)(2,1)} %param.7) | copy-start | bytes 9437188
  52.5 4.0 %copy-start.5 = (bf16[1,1,1536,1024]{3,2,1,0:T(8,128)(2,1)S(1)}, bf16[1,1,1536,1024]{3,2,1,0:T(8,128)(2,1)}, u32[]{:S(2)}) copy-start(bf16[1,1,1536,1024]{3,2,1,0:T(8,128)(2,1)} %param.8) | copy-start | bytes 9437188
  52.5 4.0 %copy-start.7 = (bf16[512,1024]{1,0:T(8,128)(2,1)S(1)}, bf16[512,1024]{1,0:T(8,128)(2,1)}, u32[]{:S(2)}) copy-start(bf16[512,1024]{1,0:T(8,128)(2,1)} %out_ref.5) | copy-start | bytes 3145732
  56.3 86.0 %collective-permute-start.3 = (f32[1024,512]{1,0:T(8,128)S(1)}, f32[1024,512]{1,0:T(8,128)S(1)}, u32[]{:S(2)}, u32[]{:S(2)}) collective-permute-start(f32[1024,512]{1,0:T(8,128)S(1)} %multiply_subtract_fusion.1.x_ref), channel_id=1, source_target_pairs={{3,0},{0,1},{1,2},{2,3},{7,4},{4,5},{5,6},{6,7},{11,8},{8,9},{9,10... | collective-permute-start | bytes 6291464 | tf_op jit(solution)/shard_map/ppermute | solution.py:19
  56.4 86.0 %collective-permute-start.2 = (f32[1024,512]{1,0:T(8,128)S(1)}, f32[1024,512]{1,0:T(8,128)S(1)}, u32[]{:S(2)}, u32[]{:S(2)}) collective-permute-start(f32[1024,512]{1,0:T(8,128)S(1)} %multiply_subtract_fusion.1.x_ref), channel_id=1, source_target_pairs={{28,0},{0,4},{4,8},{8,12},{12,16},{16,20},{20,24},{24,28},{29,1},{... | collective-permute-start | bytes 6291464 | tf_op jit(solution)/shard_map/ppermute | solution.py:19
  98.9 55.4 %collective-permute-start.6 = (f32[1024,512]{1,0:T(8,128)S(1)}, f32[1024,512]{1,0:T(8,128)S(1)}, u32[]{:S(2)}, u32[]{:S(2)}) collective-permute-start(f32[1024,512]{1,0:T(8,128)S(1)} %get-tuple-element.8.own_ref), channel_id=1, source_target_pairs={{28,0},{0,4},{4,8},{8,12},{12,16},{16,20},{20,24},{24,28},{29,1},{... | collective-permute-start | bytes 6291464 | tf_op jit(solution)/shard_map/ppermute | solution.py:19
  99.0 93.7 %collective-permute-start.9 = (f32[128,512]{1,0:T(8,128)S(1)}, f32[128,512]{1,0:T(8,128)S(1)}, u32[]{:S(2)}, u32[]{:S(2)}) collective-permute-start(f32[128,512]{1,0:T(8,128)S(1)} %get-tuple-element.13), channel_id=1, source_target_pairs={{3,0},{0,1},{1,2},{2,3},{7,4},{4,5},{5,6},{6,7},{11,8},{8,9},{9,10... | collective-permute-start | bytes 786440 | tf_op jit(solution)/shard_map/ppermute | solution.py:19
  99.0 90.8 %collective-permute-start.8 = (f32[384,512]{1,0:T(8,128)S(1)}, f32[384,512]{1,0:T(8,128)S(1)}, u32[]{:S(2)}, u32[]{:S(2)}) collective-permute-start(f32[384,512]{1,0:T(8,128)S(1)} %get-tuple-element.11), channel_id=1, source_target_pairs={{3,0},{0,1},{1,2},{2,3},{7,4},{4,5},{5,6},{6,7},{11,8},{8,9},{9,10... | collective-permute-start | bytes 2359304 | tf_op jit(solution)/shard_map/ppermute | solution.py:19
  142.3 44.1 %collective-permute-start.7 = (f32[512,512]{1,0:T(8,128)S(1)}, f32[512,512]{1,0:T(8,128)S(1)}, u32[]{:S(2)}, u32[]{:S(2)}) collective-permute-start(f32[512,512]{1,0:T(8,128)S(1)} %get-tuple-element.10), channel_id=1, source_target_pairs={{3,0},{0,1},{1,2},{2,3},{7,4},{4,5},{5,6},{6,7},{11,8},{8,9},{9,10... | collective-permute-start | bytes 3145736 | tf_op jit(solution)/shard_map/ppermute | solution.py:19
  145.4 8.9 %copy-start.1 = (f32[1024,512]{1,0:T(8,128)}, f32[1024,512]{1,0:T(8,128)S(1)}, u32[]{:S(2)}) copy-start(f32[1024,512]{1,0:T(8,128)S(1)} %multiply_subtract_fusion.x_ref) | copy-start | bytes 6291460

commit v2 on v1

--- a/solution.py
+++ b/solution.py
@@ -8,15 +8,18 @@
 from jax.sharding import PartitionSpec as P
 
 
-ITERS = 2
-
 step_rate = 0.2
 
 
-def shifted(block, axis, distance):
+def shifted(block, axis, distance, wraps=True):
     devices = range(lax.axis_size(axis))
-    route = [((i - distance) % len(devices), i) for i in devices]
+    route = [((i - distance) % len(devices), i) for i in devices if wraps or i >= distance]
     return lax.ppermute(block, axis, route)
+
+
+def last_to_second(block, axis):
+    size = lax.axis_size(axis)
+    return lax.ppermute(block, axis, [(size - 1, 1 % size)])
 
 
 def tile_of(rows, most):
@@ -114,19 +117,20 @@
     )(rest, piece)
 
 
-def tail_body(start, filled_ref, rest_ref, piece_ref, out_ref, sum_ref, sem):
-    sum_ref[...] = rest_ref[...] + piece_ref[...]
+def tail_body(start, filled_ref, rest_ref, piece_ref, far_ref, out_ref, sum_ref, sem):
+    sum_ref[...] = rest_ref[...] + piece_ref[...] + far_ref[...]
     copy = pltpu.make_async_copy(sum_ref, out_ref.at[pl.ds(start, sum_ref.shape[0])], sem)
     copy.start()
     copy.wait()
 
 
-def add_tail(filled, rest, piece, start):
+def add_tail(filled, rest, piece, far, start):
     rows, heads = piece.shape
     return pl.pallas_call(
         functools.partial(tail_body, start),
         in_specs=[
             pl.BlockSpec(memory_space=pl.ANY),
+            pl.BlockSpec(memory_space=pltpu.VMEM),
             pl.BlockSpec(memory_space=pltpu.VMEM),
             pl.BlockSpec(memory_space=pltpu.VMEM),
         ],
@@ -139,45 +143,66 @@
             flops=2 * rows * heads, bytes_accessed=12 * rows * heads, transcendentals=0
         ),
         name="add_tail",
-    )(filled, rest, piece)
-
-
-def track_body(spans, w_ref, own_ref, row_ref, col_ref, new_ref, old_ref, all_ref, *piece_refs):
+    )(filled, rest, piece, far)
+
+
+def step_sum(w, lead, own, from_row, from_col, tracker):
+    moved = w[0] * own + w[1] * from_row + w[2] * from_col - step_rate * tracker
+    return moved, moved - jnp.where(lead, step_rate * w[3], 0.0) * tracker
+
+
+def track_sum(w, lead, own, from_row, from_col, new, old):
+    tracker = w[0] * own + w[1] * from_row + w[2] * from_col + new - old
+    extra = jnp.where(lead, w[3], 0.0) * (w[0] * own + w[1] * from_row)
+    return tracker, w[2] * (tracker + extra)
+
+
+def near_sum(w, lead, own, from_row, new, old):
+    near = w[0] * own + w[1] * from_row + (new - old)
+    return near, near
+
+
+def sweep_body(formula, split, spans, w_ref, *refs):
     step = pl.program_id(0)
-    mixed = w_ref[0] * own_ref[...] + w_ref[1] * row_ref[...] + w_ref[2] * col_ref[...]
-    tracker = mixed + new_ref[...] - old_ref[...]
-    all_ref[...] = tracker
-    for (first, end), piece_ref in zip(spans, piece_refs):
+    values, at = [], 0
+    for parts in split:
+        value = refs[at][...]
+        if parts == 2:
+            value = jnp.where(step == 0, value, refs[at + 1][...])
+        values.append(value)
+        at += parts
+    result, other = formula([w_ref[i] for i in range(4)], step == 0, *values)
+    refs[at][...] = result
+    for (first, end), piece_ref in zip(spans, refs[at + 1 :]):
 
         @pl.when((step >= first) & (step < end))
         def _():
-            piece_ref[...] = w_ref[2] * tracker
-
-
-def near_body(spans, w_ref, own_ref, row_ref, new_ref, old_ref, all_ref, *piece_refs):
-    step = pl.program_id(0)
-    near = w_ref[0] * own_ref[...] + w_ref[1] * row_ref[...] + (new_ref[...] - old_ref[...])
-    all_ref[...] = near
-    for (first, end), piece_ref in zip(spans, piece_refs):
-
-        @pl.when((step >= first) & (step < end))
-        def _():
-            piece_ref[...] = near
-
-
-def sweep(body, weights, arrays, cuts, tile):
+            piece_ref[...] = other
+
+
+def sweep(formula, weights, arrays, cuts, tile):
     rows, heads = arrays[0].shape
     spans = [(a // tile, b // tile) for a, b in cuts]
 
-    def piece_spec(first, end):
+    def part(first, end):
         return pl.BlockSpec((tile, heads), lambda i: (jnp.clip(i - first, 0, end - first - 1), 0))
 
-    block = pl.BlockSpec((tile, heads), lambda i: (i, 0))
-    return pl.pallas_call(
-        functools.partial(body, spans),
-        grid=(rows // tile,),
-        in_specs=[pl.BlockSpec(memory_space=pltpu.SMEM)] + [block] * len(arrays),
-        out_specs=[block] + [piece_spec(*span) for span in spans],
+    steps = rows // tile
+    specs, flat, split = [], [], []
+    for array in arrays:
+        if isinstance(array, tuple):
+            specs += [part(0, 1), part(1, steps)]
+            flat += array
+            split.append(2)
+        else:
+            specs.append(part(0, steps))
+            flat.append(array)
+            split.append(1)
+    return pl.pallas_call(
+        functools.partial(sweep_body, formula, split, spans),
+        grid=(steps,),
+        in_specs=[pl.BlockSpec(memory_space=pltpu.SMEM)] + specs,
+        out_specs=[part(0, steps)] + [part(*span) for span in spans],
         out_shape=[jax.ShapeDtypeStruct((rows, heads), jnp.float32)]
         + [jax.ShapeDtypeStruct((b - a, heads), jnp.float32) for a, b in cuts],
         compiler_params=pltpu.CompilerParams(
@@ -186,58 +211,51 @@
         cost_estimate=pl.CostEstimate(
             flops=8 * rows * heads, bytes_accessed=28 * rows * heads, transcendentals=0
         ),
-    )(weights, *arrays)
-
-
-def combine(mix_weights, own, from_row, from_col):
-    return mix_weights[0] * own + mix_weights[1] * from_row + mix_weights[2] * from_col
+    )(weights, *flat)
 
 
 def on_device(value_proj, token_pool, target_pool, batch_ids, frozen_out, numerators):
     counts = numerators.astype(jnp.float32)
+    is_last = lax.axis_index("col") == lax.axis_size("col") - 1
     mix_weights = counts / jnp.sum(counts)
-    current = value_proj[0, 0]
-    width = current.shape[0]
-    tile = width // 8
-    cuts = [(0, width // 2), (width // 2, width - tile), (width - tile, width)]
+    weights = jnp.concatenate([mix_weights, is_last.astype(jnp.float32)[None]])
+    x0 = value_proj[0, 0]
+    width = x0.shape[0]
+    lead = width // 8
+    middle = width * 5 // 8
+    cuts = [(lead, middle), (middle, width), (0, lead)]
 
     def gradient_at(field, which):
         return local_gradient(
             which, field, token_pool[0, 0], target_pool[0, 0], batch_ids[0, 0], frozen_out
         )
 
-    def neighbours(field):
-        from_col = shifted(field, "col", 1)
-        return shifted(field, "row", 1), from_col
-
-    around_current = neighbours(current)
-    grad_old = gradient_at(current, 0)
-    tracker = grad_old
-    for which in range(1, ITERS + 1):
-        final = which == ITERS
-        if which == 1:
-            around_tracker = neighbours(tracker)
-        current = combine(mix_weights, current, *around_current) - step_rate * tracker
-        if not final:
-            around_current = neighbours(current)
-        grad_new = gradient_at(current, which)
-        if not final:
-            arrays = (tracker, *around_tracker, grad_new, grad_old)
-            ends = cuts if which == ITERS - 1 else []
-            tracker, *blocks = sweep(track_body, mix_weights, arrays, ends, tile)
-            if which < ITERS - 1:
-                around_tracker = neighbours(tracker)
-            else:
-                pieces = [shifted(b, "col", 1) for b in blocks]
-                track_row = shifted(tracker, "row", 1)
-            grad_old = grad_new
-
-    arrays = (tracker, track_row, grad_new, grad_old)
-    result, last = sweep(near_body, mix_weights, arrays, cuts[-1:], tile)
+    x0_col = shifted(x0, "col", 1)
+    x0_row = shifted(x0, "row", 1)
+    g0 = gradient_at(x0, 0)
+    g0_rest, g0_lead = lax.optimization_barrier((g0[lead:], g0[:lead]))
+    g0_col = (shifted(g0_lead, "col", 1, wraps=False), shifted(g0_rest, "col", 1))
+    g0_row = shifted(g0, "row", 1)
+
+    x1, x1_send = sweep(step_sum, weights, (x0, x0_row, x0_col, g0), [(0, width)], lead)
+    x1_col = shifted(x1_send, "col", 1)
+    x1_row = shifted(x1, "row", 1)
+    g1 = gradient_at(x1, 1)
+
+    arrays = (g0, g0_row, g0_col, g1, g0)
+    t1, *blocks = sweep(track_sum, weights, arrays, cuts, lead)
+    pieces = [shifted(block, "col", 1) for block in blocks]
+    far = last_to_second(mix_weights[2] * mix_weights[2] * g0_lead, "col")
+    t1_row = shifted(t1, "row", 1)
+
+    (x2,) = sweep(step_sum, weights, (x1, x1_row, x1_col, t1), [], lead)
+    g2 = gradient_at(x2, 2)
+
+    t2, last = sweep(near_sum, weights, (t1, t1_row, g2, g1), cuts[-1:], lead)
     for (start, _), piece in zip(cuts[:-1], pieces):
-        result = add_piece(result, piece, start)
-    result = add_tail(result, last, pieces[-1], cuts[-1][0])
-    return (current[None, None], result[None, None])
+        t2 = add_piece(t2, piece, start)
+    t2 = add_tail(t2, last, pieces[-1], far, cuts[-1][0])
+    return (x2[None, None], t2[None, None])
 
 
 def solution(mesh):

time: 194 us -> 188 us (0.969)
  waiting for transfers between devices: 130 us -> 101 us
  Pallas kernels: 39 us -> 51.9 us
  starting transfers between devices: 7.83 us -> 18 us
  other arithmetic: 8.12 us -> 1.35 us
  local copies, waits for them, and re-layouts: 8 us -> 12.5 us
    ppermute x10 -> x11, waiting for transfers between devices: 130 us -> 101 us  [shifted(): return lax.ppermute(block, axis, route)]
    pallas_call x2 -> x4, Pallas kernels: 5.23 us -> 18.3 us  [sweep(): pl.pallas_call(functools.partial(sweep_body, formula, split, spans), grid...]
    ppermute x10 -> x11, starting transfers between devices: 7.83 us -> 17.3 us  [shifted(): return lax.ppermute(block, axis, route)]
    sub x2 -> x0, other arithmetic: 6.87 us -> none  [on_device(): combine(mix_weights, current, *around_current) - step_rate * tracker]
    unnamed x19 -> x21, local copies, waits for them, and re-layouts: 7.34 us -> 10.5 us
  transfers between devices with their start and end apart: 10 -> 12, of which waited for: 4 -> 6; matrix products, arithmetic and copies ran while one was open for 5% -> 2% of each run, Pallas kernels for 20% -> 27%
where the time goes in v2:
time: 188 us; the launch traced here: 187 us
  waiting for transfers between devices  101 us (54%)
  Pallas kernels  51.9 us (28%)
  starting transfers between devices  18 us (10%)
  local copies, waits for them, and re-layouts  12.5 us (7%)
  between operations  2.11 us (1%)
    ppermute x11, waiting for transfers between devices, shifted(): return lax.ppermute(block, axis, route)  101 us
    pallas_call x3, Pallas kernels, local_gradient(): pl.pallas_call(functools.partial(gradient_body, which, tile, width ** (-0...  26.6 us
    pallas_call x4, Pallas kernels, sweep(): pl.pallas_call(functools.partial(sweep_body, formula, split, spans), grid...  18.3 us
    ppermute x11, starting transfers between devices, shifted(): return lax.ppermute(block, axis, route)  17.3 us
    unnamed x21, local copies, waits for them, and re-layouts  10.5 us
    pallas_call x2, Pallas kernels, add_piece(): pl.pallas_call(add_body, grid=(rows // tile,), in_specs=[pl.BlockSpec((ti...  6.24 us
  transfers between devices with their start and end apart: 12, of which 6 were waited for; matrix products, arithmetic and copies ran while one was open for 2% of the time, Pallas kernels for 27%

profile of v2, /device:TPU:0, one launch (start us, length us, event | category | flops | bytes accessed | tf_op | source)
XLA Modules:
  0.0 187.2 jit_solution(16340924487093481983)
XLA Ops:
  0.6 3.1 %collective-permute-start.1 = (f32[1024,512]{1,0:T(8,128)}, f32[1024,512]{1,0:T(8,128)}, u32[]{:S(2)}, u32[]{:S(2)}) collective-permute-start(f32[1024,512]{1,0:T(8,128)} %bitcast.10), channel_id=1, source_target_pairs={{3,0},{0,1},{1,2},{2,3},{7,4},{4,5},{5,6},{6,7},{11,8},{8,9},{9,10... | collective-permute-start | bytes 6291464 | tf_op jit(solution)/shard_map/ppermute | solution.py:17
  3.7 0.7 copy.13
  4.5 1.6 copy-done
  6.1 1.9 %copy-done.3 = bf16[1,1,1536,1024]{3,2,1,0:T(8,128)(2,1)S(1)} copy-done((bf16[1,1,1536,1024]{3,2,1,0:T(8,128)(2,1)S(1)}, bf16[1,1,1536,1024]{3,2,1,0:T(8,128)(2,1)}, u32[]{:S(2)}) %copy-start.3) | copy-done | bytes 3145752
  8.0 1.9 %copy-done.5 = bf16[1,1,1536,1024]{3,2,1,0:T(8,128)(2,1)S(1)} copy-done((bf16[1,1,1536,1024]{3,2,1,0:T(8,128)(2,1)S(1)}, bf16[1,1,1536,1024]{3,2,1,0:T(8,128)(2,1)}, u32[]{:S(2)}) %copy-start.5) | copy-done | bytes 3145752
  9.8 1.2 copy-done.7
  11.1 8.8 %shard_map.77.refs_3_.refs_0_.refs_5_ = f32[1024,512]{1,0:T(8,128)S(1)} custom-call(s32[3,1536]{1,0:T(4,128)S(1)} %bitcast.15, f32[1024,512]{1,0:T(8,128)S(1)} %bitcast.12, bf16[1536,1024]{1,0:T(8,128)(2,1)S(1)} %bitcast.18, bf16[1536,1024]{1,0:T(8,128)(2,1)S(1)} %bitcast.21, bf16[512,1024]{1,0:T(8,128)(2,1)S(1)} %copy-done.7), custom_call_target="tpu_custom_call" | custom-call | flops 6442450944 | bytes 12582912 | tf_op jit(solution)/shard_map/pallas_call | solution.py:72
  19.8 1.7 collective-permute-start.4
  21.5 1.4 slice.13
  22.9 1.6 collective-permute-start.6
  24.5 3.5 %collective-permute-start.5 = (f32[128,512]{1,0:T(8,128)S(1)}, f32[128,512]{1,0:T(8,128)S(1)}, u32[]{:S(2)}, u32[]{:S(2)}) collective-permute-start(f32[128,512]{1,0:T(8,128)S(1)} %slice.14), channel_id=1, source_target_pairs={{0,1},{1,2},{2,3},{4,5},{5,6},{6,7},{8,9},{9,10},{10,11},{12,13},{... | collective-permute-start | bytes 786440 | tf_op jit(solution)/shard_map/ppermute | solution.py:17
  29.3 23.2 %collective-permute-done.1.refs_2_ = f32[1024,512]{1,0:T(8,128)} collective-permute-done((f32[1024,512]{1,0:T(8,128)}, f32[1024,512]{1,0:T(8,128)}, u32[]{:S(2)}, u32[]{:S(2)}) %collective-permute-start.1) | collective-permute-done | bytes 2097184 | tf_op jit(solution)/shard_map/ppermute | solution.py:17
  52.6 1.6 copy-done.1
  54.2 5.7 %shard_map.78 = (f32[1024,512]{1,0:T(8,128)S(1)}, f32[1024,512]{1,0:T(8,128)S(1)}) custom-call(f32[4]{0:T(128)S(1)} %pad_maximum_fusion.w_ref, f32[1024,512]{1,0:T(8,128)S(1)} %bitcast.13, f32[1024,512]{1,0:T(8,128)} %collective-permute-done.refs_1_, f32[1024,512]{1,0:T(8,128)} %collective-permute-done.1.refs_2_, ...), custom_call_target="tpu_custom_call" | custom-call | flops 4194304 | bytes 14680064 | tf_op jit(solution)/shard_map/pallas_call | solution.py:201
  60.0 8.9 %shard_map.79.refs_4_.refs_3_ = f32[1024,512]{1,0:T(8,128)S(1)} custom-call(s32[3,1536]{1,0:T(4,128)S(1)} %bitcast.16, f32[1024,512]{1,0:T(8,128)S(1)} %get-tuple-element.12.x_ref.refs_0_, bf16[1536,1024]{1,0:T(8,128)(2,1)S(1)} %bitcast.19, bf16[1536,1024]{1,0:T(8,128)(2,1)S(1)} %bitcast.22, bf16[512,1024]{1,0:T(8,128)(2,1)S(1)} %copy-done.8), custom_call_target="tpu_custom_call" | custom-call | flops 6442450944 | bytes 12582912 | tf_op jit(solution)/shard_map/pallas_call | solution.py:72
  69.0 26.0 %collective-permute-done.5.refs_2_ = f32[128,512]{1,0:T(8,128)S(1)} collective-permute-done((f32[128,512]{1,0:T(8,128)S(1)}, f32[128,512]{1,0:T(8,128)S(1)}, u32[]{:S(2)}, u32[]{:S(2)}) %collective-permute-start.5) | collective-permute-done | bytes 262176 | tf_op jit(solution)/shard_map/ppermute | solution.py:17
  94.9 5.2 %shard_map.80 = (f32[1024,512]{1,0:T(8,128)S(1)}, f32[512,512]{1,0:T(8,128)S(1)}, f32[384,512]{1,0:T(8,128)S(1)}, f32[128,512]{1,0:T(8,128)S(1)}) custom-call(f32[4]{0:T(128)S(1)} %pad_maximum_fusion.w_ref, f32[1024,512]{1,0:T(8,128)S(1)} %shard_map.77.refs_3_.refs_0_.refs_5_, f32[1024,512]{1,0:T(8,128)} %collective-permute-done.4.refs_1_, ...), custom_call_target="tpu_custom_call" | custom-call | flops 4194304 | bytes 14680064 | tf_op jit(solution)/shard_map/pallas_call | solution.py:201
  100.1 2.5 %collective-permute-start.8 = (f32[512,512]{1,0:T(8,128)S(1)}, f32[512,512]{1,0:T(8,128)S(1)}, u32[]{:S(2)}, u32[]{:S(2)}) collective-permute-start(f32[512,512]{1,0:T(8,128)S(1)} %get-tuple-element.18), channel_id=1, source_target_pairs={{3,0},{0,1},{1,2},{2,3},{7,4},{4,5},{5,6},{6,7},{11,8},{8,9},{9,10... | collective-permute-start | bytes 3145736 | tf_op jit(solution)/shard_map/ppermute | solution.py:17
  104.5 1.6 collective-permute-start.9
  106.2 33.6 %collective-permute-done.3.refs_2_ = f32[1024,512]{1,0:T(8,128)S(1)} collective-permute-done((f32[1024,512]{1,0:T(8,128)S(1)}, f32[1024,512]{1,0:T(8,128)S(1)}, u32[]{:S(2)}, u32[]{:S(2)}) %collective-permute-start.3) | collective-permute-done | bytes 2097184 | tf_op jit(solution)/shard_map/ppermute | solution.py:17
  139.8 0.7 collective-permute-start.11
  140.5 3.1 %collective-permute-start.10 = (f32[128,512]{1,0:T(8,128)S(1)}, f32[128,512]{1,0:T(8,128)S(1)}, u32[]{:S(2)}, u32[]{:S(2)}) collective-permute-start(f32[128,512]{1,0:T(8,128)S(1)} %get-tuple-element.21), channel_id=1, source_target_pairs={{3,0},{0,1},{1,2},{2,3},{7,4},{4,5},{5,6},{6,7},{11,8},{8,9},{9,10... | collective-permute-start | bytes 786440 | tf_op jit(solution)/shard_map/ppermute | solution.py:17
  143.7 3.7 %shard_map.81.x_ref = f32[1024,512]{1,0:T(8,128)} custom-call(f32[4]{0:T(128)S(1)} %pad_maximum_fusion.w_ref, f32[1024,512]{1,0:T(8,128)S(1)} %get-tuple-element.12.x_ref.refs_0_, f32[1024,512]{1,0:T(8,128)S(1)} %collective-permute-done.2.refs_1_, f32[1024,512]{1,0:T(8,128)S(1)} %collective-permute-done.3.refs_2_, ...), custom_call_target="tpu_custom_call" | custom-call | flops 4194304 | bytes 14680064 | tf_op jit(solution)/shard_map/pallas_call | solution.py:201
  147.4 1.6 copy-done.2
  149.0 8.9 %shard_map.82.refs_2_ = f32[1024,512]{1,0:T(8,128)S(1)} custom-call(s32[3,1536]{1,0:T(4,128)S(1)} %bitcast.17, f32[1024,512]{1,0:T(8,128)S(1)} %copy-done.2, bf16[1536,1024]{1,0:T(8,128)(2,1)S(1)} %bitcast.20, bf16[1536,1024]{1,0:T(8,128)(2,1)S(1)} %bitcast.23, bf16[512,1024]{1,0:T(8,128)(2,1)S(1)} %copy-done.8), custom_call_target="tpu_custom_call" | custom-call | flops 6442450944 | bytes 12582912 | tf_op jit(solution)/shard_map/pallas_call | solution.py:72
  157.9 3.7 %shard_map.83 = (f32[1024,512]{1,0:T(8,128)}, f32[128,512]{1,0:T(8,128)S(1)}) custom-call(f32[4]{0:T(128)S(1)} %pad_maximum_fusion.w_ref, f32[1024,512]{1,0:T(8,128)S(1)} %get-tuple-element.16.refs_3_.refs_0_, f32[1024,512]{1,0:T(8,128)S(1)} %collective-permute-done.7.refs_1_, f32[1024,512]{1,0:T(8,128)S(1)} %shard_map.82.refs_2_, ...), custom_call_target="tpu_custom_call" | custom-call | flops 4194304 | bytes 14680064 | tf_op jit(solution)/shard_map/pallas_call | solution.py:201
  161.7 0.6 collective-permute-done.8.piece_ref
  162.3 3.4 %add_piece.2.rest_ref = f32[1024,512]{1,0:T(8,128)} custom-call(f32[1024,512]{1,0:T(8,128)} %get-tuple-element.17.rest_ref, f32[512,512]{1,0:T(8,128)S(1)} %collective-permute-done.8.piece_ref), custom_call_target="tpu_custom_call", output_to_operand_aliasing={{}: (0, {})} | custom-call | flops 524288 | bytes 3145728 | tf_op jit(solution)/shard_map/add_piece/pallas_call | solution.py:102
  165.7 13.5 %collective-permute-done.9.piece_ref = f32[384,512]{1,0:T(8,128)S(1)} collective-permute-done((f32[384,512]{1,0:T(8,128)S(1)}, f32[384,512]{1,0:T(8,128)S(1)}, u32[]{:S(2)}, u32[]{:S(2)}) %collective-permute-start.9) | collective-permute-done | bytes 786464 | tf_op jit(solution)/shard_map/ppermute | solution.py:17
  179.2 2.9 %add_piece.3.filled_ref = f32[1024,512]{1,0:T(8,128)} custom-call(f32[1024,512]{1,0:T(8,128)} %add_piece.2.rest_ref, f32[384,512]{1,0:T(8,128)S(1)} %collective-permute-done.9.piece_ref), custom_call_target="tpu_custom_call", output_to_operand_aliasing={{}: (0, {})} | custom-call | flops 393216 | bytes 2359296 | tf_op jit(solution)/shard_map/add_piece/pallas_call | solution.py:102
  182.0 4.4 %collective-permute-done.10.piece_ref = f32[128,512]{1,0:T(8,128)S(1)} collective-permute-done((f32[128,512]{1,0:T(8,128)S(1)}, f32[128,512]{1,0:T(8,128)S(1)}, u32[]{:S(2)}, u32[]{:S(2)}) %collective-permute-start.10) | collective-permute-done | bytes 262176 | tf_op jit(solution)/shard_map/ppermute | solution.py:17
  186.4 0.8 add_tail.1
  (30 shorter events, 2.2 us)
Async XLA Ops:
  0.6 51.9 %collective-permute-start.1 = (f32[1024,512]{1,0:T(8,128)}, f32[1024,512]{1,0:T(8,128)}, u32[]{:S(2)}, u32[]{:S(2)}) collective-permute-start(f32[1024,512]{1,0:T(8,128)} %bitcast.10), channel_id=1, source_target_pairs={{3,0},{0,1},{1,2},{2,3},{7,4},{4,5},{5,6},{6,7},{11,8},{8,9},{9,10... | collective-permute-start | bytes 6291464 | tf_op jit(solution)/shard_map/ppermute | solution.py:17
  3.7 48.8 %collective-permute-start = (f32[1024,512]{1,0:T(8,128)}, f32[1024,512]{1,0:T(8,128)}, u32[]{:S(2)}, u32[]{:S(2)}) collective-permute-start(f32[1024,512]{1,0:T(8,128)} %bitcast.11), channel_id=1, source_target_pairs={{28,0},{0,4},{4,8},{8,12},{12,16},{16,20},{20,24},{24,28},{29,1},{... | collective-permute-start | bytes 6291464 | tf_op jit(solution)/shard_map/ppermute | solution.py:17
  4.5 1.6 copy-start
  6.1 1.9 %copy-start.3 = (bf16[1,1,1536,1024]{3,2,1,0:T(8,128)(2,1)S(1)}, bf16[1,1,1536,1024]{3,2,1,0:T(8,128)(2,1)}, u32[]{:S(2)}) copy-start(bf16[1,1,1536,1024]{3,2,1,0:T(8,128)(2,1)} %param.7) | copy-start | bytes 9437188
  7.9 1.9 %copy-start.5 = (bf16[1,1,1536,1024]{3,2,1,0:T(8,128)(2,1)S(1)}, bf16[1,1,1536,1024]{3,2,1,0:T(8,128)(2,1)}, u32[]{:S(2)}) copy-start(bf16[1,1,1536,1024]{3,2,1,0:T(8,128)(2,1)} %param.8) | copy-start | bytes 9437188
  9.8 1.2 copy-start.7
  19.8 8.1 %copy-start.9 = (s32[3]{0:T(128)S(1)}, s32[3]{0:T(128)}, u32[]{:S(2)}) copy-start(s32[3]{0:T(128)} %param.11) | copy-start | bytes 40
  19.8 75.1 %collective-permute-start.4 = (f32[1024,512]{1,0:T(8,128)S(1)}, f32[1024,512]{1,0:T(8,128)}, u32[]{:S(2)}, u32[]{:S(2)}) collective-permute-start(f32[1024,512]{1,0:T(8,128)S(1)} %shard_map.77.refs_3_.refs_0_.refs_5_), channel_id=1, source_target_pairs={{28,0},{0,4},{4,8},{8,12},{12,16},{16,20},{20,24},{24,28},{29,1},{... | collective-permute-start | bytes 6291464 | tf_op jit(solution)/shard_map/ppermute | solution.py:17
  22.9 72.0 %collective-permute-start.6 = (f32[896,512]{1,0:T(8,128)}, f32[896,512]{1,0:T(8,128)}, u32[]{:S(2)}, u32[]{:S(2)}) collective-permute-start(f32[896,512]{1,0:T(8,128)} %slice.13), channel_id=1, source_target_pairs={{3,0},{0,1},{1,2},{2,3},{7,4},{4,5},{5,6},{6,7},{11,8},{8,9},{9,10... | collective-permute-start | bytes 5505032 | tf_op jit(solution)/shard_map/ppermute | solution.py:17
  24.5 70.4 %collective-permute-start.5 = (f32[128,512]{1,0:T(8,128)S(1)}, f32[128,512]{1,0:T(8,128)S(1)}, u32[]{:S(2)}, u32[]{:S(2)}) collective-permute-start(f32[128,512]{1,0:T(8,128)S(1)} %slice.14), channel_id=1, source_target_pairs={{0,1},{1,2},{2,3},{4,5},{5,6},{6,7},{8,9},{9,10},{10,11},{12,13},{... | collective-permute-start | bytes 786440 | tf_op jit(solution)/shard_map/ppermute | solution.py:17
  52.6 1.6 copy-start.1
  54.2 5.8 %copy-start.4 = (bf16[1,1,1536,1024]{3,2,1,0:T(8,128)(2,1)S(1)}, bf16[1,1,1536,1024]{3,2,1,0:T(8,128)(2,1)}, u32[]{:S(2)}) copy-start(bf16[1,1,1536,1024]{3,2,1,0:T(8,128)(2,1)} %param.7) | copy-start | bytes 9437188
  54.2 5.8 %copy-start.6 = (bf16[1,1,1536,1024]{3,2,1,0:T(8,128)(2,1)S(1)}, bf16[1,1,1536,1024]{3,2,1,0:T(8,128)(2,1)}, u32[]{:S(2)}) copy-start(bf16[1,1,1536,1024]{3,2,1,0:T(8,128)(2,1)} %param.8) | copy-start | bytes 9437188
  54.2 5.8 %copy-start.8 = (bf16[512,1024]{1,0:T(8,128)(2,1)S(1)}, bf16[512,1024]{1,0:T(8,128)(2,1)}, u32[]{:S(2)}) copy-start(bf16[512,1024]{1,0:T(8,128)(2,1)} %out_ref.5) | copy-start | bytes 3145732
  59.8 80.0 %collective-permute-start.3 = (f32[1024,512]{1,0:T(8,128)S(1)}, f32[1024,512]{1,0:T(8,128)S(1)}, u32[]{:S(2)}, u32[]{:S(2)}) collective-permute-start(f32[1024,512]{1,0:T(8,128)S(1)} %get-tuple-element.13), channel_id=1, source_target_pairs={{3,0},{0,1},{1,2},{2,3},{7,4},{4,5},{5,6},{6,7},{11,8},{8,9},{9,10... | collective-permute-start | bytes 6291464 | tf_op jit(solution)/shard_map/ppermute | solution.py:17
  59.9 80.6 %collective-permute-start.2 = (f32[1024,512]{1,0:T(8,128)S(1)}, f32[1024,512]{1,0:T(8,128)S(1)}, u32[]{:S(2)}, u32[]{:S(2)}) collective-permute-start(f32[1024,512]{1,0:T(8,128)S(1)} %get-tuple-element.12.x_ref.refs_0_), channel_id=1, source_target_pairs={{28,0},{0,4},{4,8},{8,12},{12,16},{16,20},{20,24},{24,28},{29,1},{... | collective-permute-start | bytes 6291464 | tf_op jit(solution)/shard_map/ppermute | solution.py:17
  100.1 57.9 %collective-permute-start.7 = (f32[1024,512]{1,0:T(8,128)S(1)}, f32[1024,512]{1,0:T(8,128)S(1)}, u32[]{:S(2)}, u32[]{:S(2)}) collective-permute-start(f32[1024,512]{1,0:T(8,128)S(1)} %get-tuple-element.16.refs_3_.refs_0_), channel_id=1, source_target_pairs={{28,0},{0,4},{4,8},{8,12},{12,16},{16,20},{20,24},{24,28},{29,1},{... | collective-permute-start | bytes 6291464 | tf_op jit(solution)/shard_map/ppermute | solution.py:17
  100.1 62.2 %collective-permute-start.8 = (f32[512,512]{1,0:T(8,128)S(1)}, f32[512,512]{1,0:T(8,128)S(1)}, u32[]{:S(2)}, u32[]{:S(2)}) collective-permute-start(f32[512,512]{1,0:T(8,128)S(1)} %get-tuple-element.18), channel_id=1, source_target_pairs={{3,0},{0,1},{1,2},{2,3},{7,4},{4,5},{5,6},{6,7},{11,8},{8,9},{9,10... | collective-permute-start | bytes 3145736 | tf_op jit(solution)/shard_map/ppermute | solution.py:17
  104.5 74.6 %collective-permute-start.9 = (f32[384,512]{1,0:T(8,128)S(1)}, f32[384,512]{1,0:T(8,128)S(1)}, u32[]{:S(2)}, u32[]{:S(2)}) collective-permute-start(f32[384,512]{1,0:T(8,128)S(1)} %get-tuple-element.19), channel_id=1, source_target_pairs={{3,0},{0,1},{1,2},{2,3},{7,4},{4,5},{5,6},{6,7},{11,8},{8,9},{9,10... | collective-permute-start | bytes 2359304 | tf_op jit(solution)/shard_map/ppermute | solution.py:17
  139.8 42.2 %collective-permute-start.11 = (f32[128,512]{1,0:T(8,128)S(1)}, f32[128,512]{1,0:T(8,128)S(1)}, u32[]{:S(2)}, u32[]{:S(2)}) collective-permute-start(f32[128,512]{1,0:T(8,128)S(1)} %broadcast_multiply_fusion), channel_id=1, source_target_pairs={{3,1},{7,5},{11,9},{15,13},{19,17},{23,21},{27,25},{31,29}} | collective-permute-start | bytes 786440 | tf_op jit(solution)/shard_map/ppermute | solution.py:22
  140.5 45.9 %collective-permute-start.10 = (f32[128,512]{1,0:T(8,128)S(1)}, f32[128,512]{1,0:T(8,128)S(1)}, u32[]{:S(2)}, u32[]{:S(2)}) collective-permute-start(f32[128,512]{1,0:T(8,128)S(1)} %get-tuple-element.21), channel_id=1, source_target_pairs={{3,0},{0,1},{1,2},{2,3},{7,4},{4,5},{5,6},{6,7},{11,8},{8,9},{9,10... | collective-permute-start | bytes 786440 | tf_op jit(solution)/shard_map/ppermute | solution.py:17
  147.4 1.6 copy-start.2

commit v3 on v2

--- a/solution.py
+++ b/solution.py
@@ -9,6 +9,8 @@
 
 
 step_rate = 0.2
+
+SUMS_VMEM = 24 * 2**20
 
 
 def shifted(block, axis, distance, wraps=True):
@@ -83,7 +85,7 @@
         out_shape=jax.ShapeDtypeStruct((width, heads), jnp.float32),
         scratch_shapes=[pltpu.VMEM(current.shape, jnp.bfloat16)],
         compiler_params=pltpu.CompilerParams(
-            dimension_semantics=("arbitrary",), vmem_limit_bytes=32 * 2**20
+            dimension_semantics=("arbitrary",), vmem_limit_bytes=20 * 2**20
         ),
         cost_estimate=pl.CostEstimate(
             flops=8 * pool * width * heads, bytes_accessed=12 * 2**20, transcendentals=0
@@ -148,70 +150,86 @@
 
 def step_sum(w, lead, own, from_row, from_col, tracker):
     moved = w[0] * own + w[1] * from_row + w[2] * from_col - step_rate * tracker
-    return moved, moved - jnp.where(lead, step_rate * w[3], 0.0) * tracker
+    return moved, moved - step_rate * w[3] * tracker if lead else moved
+
+
+def plain_step(w, lead, own, from_row, from_col, tracker):
+    return (step_sum(w, False, own, from_row, from_col, tracker)[0],) * 2
 
 
 def track_sum(w, lead, own, from_row, from_col, new, old):
     tracker = w[0] * own + w[1] * from_row + w[2] * from_col + new - old
-    extra = jnp.where(lead, w[3], 0.0) * (w[0] * own + w[1] * from_row)
+    extra = w[3] * (w[0] * own + w[1] * from_row) if lead else 0.0
     return tracker, w[2] * (tracker + extra)
 
 
-def near_sum(w, lead, own, from_row, new, old):
-    near = w[0] * own + w[1] * from_row + (new - old)
-    return near, near
-
-
-def sweep_body(formula, split, spans, w_ref, *refs):
-    step = pl.program_id(0)
-    values, at = [], 0
-    for parts in split:
-        value = refs[at][...]
-        if parts == 2:
-            value = jnp.where(step == 0, value, refs[at + 1][...])
-        values.append(value)
-        at += parts
-    result, other = formula([w_ref[i] for i in range(4)], step == 0, *values)
-    refs[at][...] = result
-    for (first, end), piece_ref in zip(spans, refs[at + 1 :]):
-
-        @pl.when((step >= first) & (step < end))
-        def _():
-            piece_ref[...] = other
-
-
-def sweep(formula, weights, arrays, cuts, tile):
+def sums_body(formula, split, cuts, tile, w_ref, *refs):
+    w = [w_ref[i] for i in range(4)]
+    first_out = sum(split)
+    for start in range(0, refs[first_out].shape[0], tile):
+        values, at = [], 0
+        for parts in split:
+            if parts == 1:
+                values.append(refs[at][pl.ds(start, tile)])
+            elif start == 0:
+                values.append(refs[at][...])
+            else:
+                values.append(refs[at + 1][pl.ds(start - tile, tile)])
+            at += parts
+        result, other = formula(w, start == 0, *values)
+        refs[at][pl.ds(start, tile)] = result
+        for (a, b), piece_ref in zip(cuts, refs[at + 1 :]):
+            if a <= start < b:
+                piece_ref[pl.ds(start - a, tile)] = other
+
+
+def sums(formula, weights, arrays, cuts, tile):
     rows, heads = arrays[0].shape
-    spans = [(a // tile, b // tile) for a, b in cuts]
-
-    def part(first, end):
-        return pl.BlockSpec((tile, heads), lambda i: (jnp.clip(i - first, 0, end - first - 1), 0))
-
-    steps = rows // tile
-    specs, flat, split = [], [], []
-    for array in arrays:
-        if isinstance(array, tuple):
-            specs += [part(0, 1), part(1, steps)]
-            flat += array
-            split.append(2)
-        else:
-            specs.append(part(0, steps))
-            flat.append(array)
-            split.append(1)
-    return pl.pallas_call(
-        functools.partial(sweep_body, formula, split, spans),
-        grid=(steps,),
-        in_specs=[pl.BlockSpec(memory_space=pltpu.SMEM)] + specs,
-        out_specs=[part(0, steps)] + [part(*span) for span in spans],
+    split = [len(array) if isinstance(array, tuple) else 1 for array in arrays]
+    flat = jax.tree.leaves(list(arrays))
+    held = pl.BlockSpec(memory_space=pltpu.VMEM)
+    return pl.pallas_call(
+        functools.partial(sums_body, formula, split, cuts, tile),
+        in_specs=[pl.BlockSpec(memory_space=pltpu.SMEM)] + [held] * len(flat),
+        out_specs=[held] * (1 + len(cuts)),
         out_shape=[jax.ShapeDtypeStruct((rows, heads), jnp.float32)]
         + [jax.ShapeDtypeStruct((b - a, heads), jnp.float32) for a, b in cuts],
+        compiler_params=pltpu.CompilerParams(vmem_limit_bytes=SUMS_VMEM),
+        cost_estimate=pl.CostEstimate(
+            flops=8 * rows * heads, bytes_accessed=28 * rows * heads, transcendentals=0
+        ),
+    )(weights, *flat)
+
+
+def near_body(w_ref, own_ref, row_ref, new_ref, old_ref, near_ref, lead_ref):
+    near = w_ref[0] * own_ref[...] + w_ref[1] * row_ref[...] + (new_ref[...] - old_ref[...])
+    near_ref[...] = near
+
+    @pl.when(pl.program_id(0) == 0)
+    def _():
+        lead_ref[...] = near
+
+
+def near_sums(weights, arrays, tile):
+    rows, heads = arrays[0].shape
+    block = pl.BlockSpec((tile, heads), lambda i: (i, 0))
+    return pl.pallas_call(
+        near_body,
+        grid=(rows // tile,),
+        in_specs=[pl.BlockSpec(memory_space=pltpu.SMEM)] + [block] * len(arrays),
+        out_specs=[block, pl.BlockSpec((tile, heads), lambda i: (0, 0))],
+        out_shape=[
+            jax.ShapeDtypeStruct((rows, heads), jnp.float32),
+            jax.ShapeDtypeStruct((tile, heads), jnp.float32),
+        ],
         compiler_params=pltpu.CompilerParams(
             dimension_semantics=("arbitrary",), vmem_limit_bytes=8 * 2**20
         ),
         cost_estimate=pl.CostEstimate(
-            flops=8 * rows * heads, bytes_accessed=28 * rows * heads, transcendentals=0
-        ),
-    )(weights, *flat)
+            flops=8 * rows * heads, bytes_accessed=24 * rows * heads, transcendentals=0
+        ),
+        name="near",
+    )(weights, *arrays)
 
 
 def on_device(value_proj, token_pool, target_pool, batch_ids, frozen_out, numerators):
@@ -237,25 +255,25 @@
     g0_col = (shifted(g0_lead, "col", 1, wraps=False), shifted(g0_rest, "col", 1))
     g0_row = shifted(g0, "row", 1)
 
-    x1, x1_send = sweep(step_sum, weights, (x0, x0_row, x0_col, g0), [(0, width)], lead)
+    x1, x1_send = sums(step_sum, weights, (x0, x0_row, x0_col, g0), [(0, width)], lead)
     x1_col = shifted(x1_send, "col", 1)
     x1_row = shifted(x1, "row", 1)
     g1 = gradient_at(x1, 1)
 
     arrays = (g0, g0_row, g0_col, g1, g0)
-    t1, *blocks = sweep(track_sum, weights, arrays, cuts, lead)
+    t1, *blocks = sums(track_sum, weights, arrays, cuts, lead)
     pieces = [shifted(block, "col", 1) for block in blocks]
     far = last_to_second(mix_weights[2] * mix_weights[2] * g0_lead, "col")
     t1_row = shifted(t1, "row", 1)
 
-    (x2,) = sweep(step_sum, weights, (x1, x1_row, x1_col, t1), [], lead)
+    x2, x2_out = sums(plain_step, weights, (x1, x1_row, x1_col, t1), [(0, width)], lead)
     g2 = gradient_at(x2, 2)
 
-    t2, last = sweep(near_sum, weights, (t1, t1_row, g2, g1), cuts[-1:], lead)
+    t2, last = near_sums(weights, (t1, t1_row, g2, g1), lead)
     for (start, _), piece in zip(cuts[:-1], pieces):
         t2 = add_piece(t2, piece, start)
     t2 = add_tail(t2, last, pieces[-1], far, cuts[-1][0])
-    return (x2[None, None], t2[None, None])
+    return (x2_out[None, None], t2[None, None])
 
 
 def solution(mesh):

time: 188 us -> 188 us (level)
  waiting for transfers between devices: 101 us -> 108 us
  Pallas kernels: 51.9 us -> 45.3 us
  starting transfers between devices: 18 us -> 20.1 us
    pallas_call x4, Pallas kernels: 18.3 us -> 11.8 us  [the longest x3 7.99 us: sums(): pl.pallas_call(functools.partial(sums_body, formula, split, cuts, tile),...]
    ppermute x11, waiting for transfers between devices: 101 us -> 108 us  [shifted(): return lax.ppermute(block, axis, route)]
    ppermute x11, starting transfers between devices: 17.3 us -> 19.4 us  [shifted(): return lax.ppermute(block, axis, route)]
    unnamed x21 -> x19, local copies, waits for them, and re-layouts: 10.5 us -> 8.93 us
  transfers between devices with their start and end apart: 12 -> 12, of which waited for: 6 -> 6; matrix products, arithmetic and copies ran while one was open for 2% -> 2% of each run, Pallas kernels for 27% -> 24%
where the time goes in v3:
time: 188 us; the launch traced here: 187 us
  waiting for transfers between devices  108 us (57%)
  Pallas kernels  45.3 us (24%)
  starting transfers between devices  20.1 us (11%)
  local copies, waits for them, and re-layouts  10.9 us (6%)
  between operations  2.06 us (1%)
    ppermute x11, waiting for transfers between devices, shifted(): return lax.ppermute(block, axis, route)  108 us
    pallas_call x3, Pallas kernels, local_gradient(): pl.pallas_call(functools.partial(gradient_body, which, tile, width ** (-0...  26.5 us
    ppermute x11, starting transfers between devices, shifted(): return lax.ppermute(block, axis, route)  19.4 us
    unnamed x19, local copies, waits for them, and re-layouts  8.93 us
    pallas_call x3, Pallas kernels, sums(): pl.pallas_call(functools.partial(sums_body, formula, split, cuts, tile),...  7.99 us
    pallas_call x2, Pallas kernels, add_piece(): pl.pallas_call(add_body, grid=(rows // tile,), in_specs=[pl.BlockSpec((ti...  6.25 us
    pallas_call x1, Pallas kernels, near_sums(): pl.pallas_call(near_body, grid=(rows // tile,), in_specs=[pl.BlockSpec(me...  3.77 us
  transfers between devices with their start and end apart: 12, of which 6 were waited for; matrix products, arithmetic and copies ran while one was open for 2% of the time, Pallas kernels for 24%

profile of v3, /device:TPU:0, one launch (start us, length us, event | category | flops | bytes accessed | tf_op | source)
XLA Modules:
  0.0 187.2 jit_solution(274997850786636674)
XLA Ops:
  1.2 2.6 %collective-permute-start.1 = (f32[1024,512]{1,0:T(8,128)}, f32[1024,512]{1,0:T(8,128)}, u32[]{:S(2)}, u32[]{:S(2)}) collective-permute-start(f32[1024,512]{1,0:T(8,128)} %bitcast.11), channel_id=1, source_target_pairs={{3,0},{0,1},{1,2},{2,3},{7,4},{4,5},{5,6},{6,7},{11,8},{8,9},{9,10... | collective-permute-start | bytes 6291464 | tf_op jit(solution)/shard_map/ppermute | solution.py:19
  3.8 0.7 copy.13
  4.5 1.6 copy-done
  6.1 1.9 %copy-done.2 = bf16[1,1,1536,1024]{3,2,1,0:T(8,128)(2,1)S(1)} copy-done((bf16[1,1,1536,1024]{3,2,1,0:T(8,128)(2,1)S(1)}, bf16[1,1,1536,1024]{3,2,1,0:T(8,128)(2,1)}, u32[]{:S(2)}) %copy-start.2) | copy-done | bytes 3145752
  8.0 1.9 %copy-done.4 = bf16[1,1,1536,1024]{3,2,1,0:T(8,128)(2,1)S(1)} copy-done((bf16[1,1,1536,1024]{3,2,1,0:T(8,128)(2,1)S(1)}, bf16[1,1,1536,1024]{3,2,1,0:T(8,128)(2,1)}, u32[]{:S(2)}) %copy-start.4) | copy-done | bytes 3145752
  9.9 1.2 copy-done.6
  11.1 8.8 %shard_map.77.refs_3_.refs_0_.refs_5_ = f32[1024,512]{1,0:T(8,128)S(1)} custom-call(s32[3,1536]{1,0:T(4,128)S(1)} %bitcast.14, f32[1024,512]{1,0:T(8,128)S(1)} %bitcast.12, bf16[1536,1024]{1,0:T(8,128)(2,1)S(1)} %bitcast.17, bf16[1536,1024]{1,0:T(8,128)(2,1)S(1)} %bitcast.20, bf16[512,1024]{1,0:T(8,128)(2,1)S(1)} %copy-done.6), custom_call_target="tpu_custom_call" | custom-call | flops 6442450944 | bytes 12582912 | tf_op jit(solution)/shard_map/pallas_call | solution.py:74
  19.9 1.3 collective-permute-start.4
  21.2 1.4 slice.13
  22.6 1.6 collective-permute-start.6
  24.2 3.5 %collective-permute-start.5 = (f32[128,512]{1,0:T(8,128)S(1)}, f32[128,512]{1,0:T(8,128)S(1)}, u32[]{:S(2)}, u32[]{:S(2)}) collective-permute-start(f32[128,512]{1,0:T(8,128)S(1)} %slice.14), channel_id=1, source_target_pairs={{0,1},{1,2},{2,3},{4,5},{5,6},{6,7},{8,9},{9,10},{10,11},{12,13},{... | collective-permute-start | bytes 786440 | tf_op jit(solution)/shard_map/ppermute | solution.py:19
  29.1 22.7 %collective-permute-done.1.refs_2_ = f32[1024,512]{1,0:T(8,128)} collective-permute-done((f32[1024,512]{1,0:T(8,128)}, f32[1024,512]{1,0:T(8,128)}, u32[]{:S(2)}, u32[]{:S(2)}) %collective-permute-start.1) | collective-permute-done | bytes 2097184 | tf_op jit(solution)/shard_map/ppermute | solution.py:19
  51.8 1.6 copy-done.1
  53.4 2.9 %shard_map.78 = (f32[1024,512]{1,0:T(8,128)S(1)}, f32[1024,512]{1,0:T(8,128)S(1)}) custom-call(f32[4]{0:T(128)S(1)} %pad_maximum_fusion.w_ref, f32[1024,512]{1,0:T(8,128)S(1)} %bitcast.13, f32[1024,512]{1,0:T(8,128)} %collective-permute-done.refs_1_, f32[1024,512]{1,0:T(8,128)} %collective-permute-done.1.refs_2_, ...), custom_call_target="tpu_custom_call" | custom-call | flops 4194304 | bytes 14680064 | tf_op jit(solution)/shard_map/pallas_call | solution.py:191
  56.2 1.9 %collective-permute-start.2 = (f32[1024,512]{1,0:T(8,128)S(1)}, f32[1024,512]{1,0:T(8,128)S(1)}, u32[]{:S(2)}, u32[]{:S(2)}) collective-permute-start(f32[1024,512]{1,0:T(8,128)S(1)} %get-tuple-element.14.x_ref.refs_0_), channel_id=1, source_target_pairs={{28,0},{0,4},{4,8},{8,12},{12,16},{16,20},{20,24},{24,28},{29,1},{... | collective-permute-start | bytes 6291464 | tf_op jit(solution)/shard_map/ppermute | solution.py:19
  58.2 8.9 %shard_map.79.refs_4_.old_ref = f32[1024,512]{1,0:T(8,128)S(1)} custom-call(s32[3,1536]{1,0:T(4,128)S(1)} %bitcast.15, f32[1024,512]{1,0:T(8,128)S(1)} %get-tuple-element.14.x_ref.refs_0_, bf16[1536,1024]{1,0:T(8,128)(2,1)S(1)} %bitcast.18, bf16[1536,1024]{1,0:T(8,128)(2,1)S(1)} %bitcast.21, bf16[512,1024]{1,0:T(8,128)(2,1)S(1)} %copy-done.7), custom_call_target="tpu_custom_call" | custom-call | flops 6442450944 | bytes 12582912 | tf_op jit(solution)/shard_map/pallas_call | solution.py:74
  67.1 27.3 %collective-permute-done.5.refs_2_ = f32[128,512]{1,0:T(8,128)S(1)} collective-permute-done((f32[128,512]{1,0:T(8,128)S(1)}, f32[128,512]{1,0:T(8,128)S(1)}, u32[]{:S(2)}, u32[]{:S(2)}) %collective-permute-start.5) | collective-permute-done | bytes 262176 | tf_op jit(solution)/shard_map/ppermute | solution.py:19
  94.4 2.8 %shard_map.80 = (f32[1024,512]{1,0:T(8,128)S(1)}, f32[512,512]{1,0:T(8,128)S(1)}, f32[384,512]{1,0:T(8,128)S(1)}, f32[128,512]{1,0:T(8,128)S(1)}) custom-call(f32[4]{0:T(128)S(1)} %pad_maximum_fusion.w_ref, f32[1024,512]{1,0:T(8,128)S(1)} %shard_map.77.refs_3_.refs_0_.refs_5_, f32[1024,512]{1,0:T(8,128)} %collective-permute-done.4.refs_1_, ...), custom_call_target="tpu_custom_call" | custom-call | flops 4194304 | bytes 14680064 | tf_op jit(solution)/shard_map/pallas_call | solution.py:191
  97.2 1.3 collective-permute-start.7
  98.5 2.5 %collective-permute-start.8 = (f32[512,512]{1,0:T(8,128)S(1)}, f32[512,512]{1,0:T(8,128)S(1)}, u32[]{:S(2)}, u32[]{:S(2)}) collective-permute-start(f32[512,512]{1,0:T(8,128)S(1)} %get-tuple-element.22), channel_id=1, source_target_pairs={{3,0},{0,1},{1,2},{2,3},{7,4},{4,5},{5,6},{6,7},{11,8},{8,9},{9,10... | collective-permute-start | bytes 3145736 | tf_op jit(solution)/shard_map/ppermute | solution.py:19
  102.9 1.6 collective-permute-start.9
  105.2 34.1 %collective-permute-done.3.refs_2_ = f32[1024,512]{1,0:T(8,128)S(1)} collective-permute-done((f32[1024,512]{1,0:T(8,128)S(1)}, f32[1024,512]{1,0:T(8,128)S(1)}, u32[]{:S(2)}, u32[]{:S(2)}) %collective-permute-start.3) | collective-permute-done | bytes 2097184 | tf_op jit(solution)/shard_map/ppermute | solution.py:19
  139.3 2.5 %collective-permute-start.10 = (f32[128,512]{1,0:T(8,128)S(1)}, f32[128,512]{1,0:T(8,128)S(1)}, u32[]{:S(2)}, u32[]{:S(2)}) collective-permute-start(f32[128,512]{1,0:T(8,128)S(1)} %get-tuple-element.25), channel_id=1, source_target_pairs={{3,0},{0,1},{1,2},{2,3},{7,4},{4,5},{5,6},{6,7},{11,8},{8,9},{9,10... | collective-permute-start | bytes 786440 | tf_op jit(solution)/shard_map/ppermute | solution.py:19
  141.8 2.3 %shard_map.81 = (f32[1024,512]{1,0:T(8,128)S(1)}, f32[1024,512]{1,0:T(8,128)}) custom-call(f32[4]{0:T(128)S(1)} %pad_maximum_fusion.w_ref, f32[1024,512]{1,0:T(8,128)S(1)} %get-tuple-element.14.x_ref.refs_0_, f32[1024,512]{1,0:T(8,128)S(1)} %collective-permute-done.2.refs_1_, f32[1024,512]{1,0:T(8,128)S(1)} %collective-permute-done.3.refs_2_, ...), custom_call_target="tpu_custom_call" | custom-call | flops 4194304 | bytes 14680064 | tf_op jit(solution)/shard_map/pallas_call | solution.py:191
  144.2 8.9 %shard_map.82.new_ref = f32[1024,512]{1,0:T(8,128)S(1)} custom-call(s32[3,1536]{1,0:T(4,128)S(1)} %bitcast.16, f32[1024,512]{1,0:T(8,128)S(1)} %get-tuple-element.20.x_ref, bf16[1536,1024]{1,0:T(8,128)(2,1)S(1)} %bitcast.19, bf16[1536,1024]{1,0:T(8,128)(2,1)S(1)} %bitcast.22, bf16[512,1024]{1,0:T(8,128)(2,1)S(1)} %copy-done.7), custom_call_target="tpu_custom_call" | custom-call | flops 6442450944 | bytes 12582912 | tf_op jit(solution)/shard_map/pallas_call | solution.py:74
  153.1 3.8 %near.1 = (f32[1024,512]{1,0:T(8,128)}, f32[128,512]{1,0:T(8,128)S(1)}) custom-call(f32[4]{0:T(128)S(1)} %pad_maximum_fusion.w_ref, f32[1024,512]{1,0:T(8,128)S(1)} %get-tuple-element.18.refs_3_.own_ref, f32[1024,512]{1,0:T(8,128)S(1)} %collective-permute-done.7.row_ref, f32[1024,512]{1,0:T(8,128)S(1)} %shard_map.82.new_ref, ...), custom_call_target="tpu_custom_call" | custom-call | flops 4194304 | bytes 12582912 | tf_op jit(solution)/shard_map/near/pallas_call | solution.py:216
  156.9 5.0 %collective-permute-done.8.piece_ref = f32[512,512]{1,0:T(8,128)S(1)} collective-permute-done((f32[512,512]{1,0:T(8,128)S(1)}, f32[512,512]{1,0:T(8,128)S(1)}, u32[]{:S(2)}, u32[]{:S(2)}) %collective-permute-start.8) | collective-permute-done | bytes 1048608 | tf_op jit(solution)/shard_map/ppermute | solution.py:19
  161.8 3.4 %add_piece.2.rest_ref = f32[1024,512]{1,0:T(8,128)} custom-call(f32[1024,512]{1,0:T(8,128)} %get-tuple-element.21.rest_ref, f32[512,512]{1,0:T(8,128)S(1)} %collective-permute-done.8.piece_ref), custom_call_target="tpu_custom_call", output_to_operand_aliasing={{}: (0, {})} | custom-call | flops 524288 | bytes 3145728 | tf_op jit(solution)/shard_map/add_piece/pallas_call | solution.py:104
  165.2 13.5 %collective-permute-done.9.piece_ref = f32[384,512]{1,0:T(8,128)S(1)} collective-permute-done((f32[384,512]{1,0:T(8,128)S(1)}, f32[384,512]{1,0:T(8,128)S(1)}, u32[]{:S(2)}, u32[]{:S(2)}) %collective-permute-start.9) | collective-permute-done | bytes 786464 | tf_op jit(solution)/shard_map/ppermute | solution.py:19
  178.7 2.9 %add_piece.3.filled_ref = f32[1024,512]{1,0:T(8,128)} custom-call(f32[1024,512]{1,0:T(8,128)} %add_piece.2.rest_ref, f32[384,512]{1,0:T(8,128)S(1)} %collective-permute-done.9.piece_ref), custom_call_target="tpu_custom_call", output_to_operand_aliasing={{}: (0, {})} | custom-call | flops 393216 | bytes 2359296 | tf_op jit(solution)/shard_map/add_piece/pallas_call | solution.py:104
  181.5 4.9 %collective-permute-done.10.piece_ref = f32[128,512]{1,0:T(8,128)S(1)} collective-permute-done((f32[128,512]{1,0:T(8,128)S(1)}, f32[128,512]{1,0:T(8,128)S(1)}, u32[]{:S(2)}, u32[]{:S(2)}) %collective-permute-start.10) | collective-permute-done | bytes 262176 | tf_op jit(solution)/shard_map/ppermute | solution.py:19
  186.5 0.8 add_tail.1
  (28 shorter events, 3.2 us)
Async XLA Ops:
  0.6 28.5 %collective-permute-start = (f32[1024,512]{1,0:T(8,128)}, f32[1024,512]{1,0:T(8,128)}, u32[]{:S(2)}, u32[]{:S(2)}) collective-permute-start(f32[1024,512]{1,0:T(8,128)} %bitcast.10), channel_id=1, source_target_pairs={{28,0},{0,4},{4,8},{8,12},{12,16},{16,20},{20,24},{24,28},{29,1},{... | collective-permute-start | bytes 6291464 | tf_op jit(solution)/shard_map/ppermute | solution.py:19
  1.2 50.6 %collective-permute-start.1 = (f32[1024,512]{1,0:T(8,128)}, f32[1024,512]{1,0:T(8,128)}, u32[]{:S(2)}, u32[]{:S(2)}) collective-permute-start(f32[1024,512]{1,0:T(8,128)} %bitcast.11), channel_id=1, source_target_pairs={{3,0},{0,1},{1,2},{2,3},{7,4},{4,5},{5,6},{6,7},{11,8},{8,9},{9,10... | collective-permute-start | bytes 6291464 | tf_op jit(solution)/shard_map/ppermute | solution.py:19
  4.5 1.6 copy-start
  6.1 1.9 %copy-start.2 = (bf16[1,1,1536,1024]{3,2,1,0:T(8,128)(2,1)S(1)}, bf16[1,1,1536,1024]{3,2,1,0:T(8,128)(2,1)}, u32[]{:S(2)}) copy-start(bf16[1,1,1536,1024]{3,2,1,0:T(8,128)(2,1)} %param.7) | copy-start | bytes 9437188
  8.0 1.9 %copy-start.4 = (bf16[1,1,1536,1024]{3,2,1,0:T(8,128)(2,1)S(1)}, bf16[1,1,1536,1024]{3,2,1,0:T(8,128)(2,1)}, u32[]{:S(2)}) copy-start(bf16[1,1,1536,1024]{3,2,1,0:T(8,128)(2,1)} %param.8) | copy-start | bytes 9437188
  9.9 1.2 copy-start.6
  19.9 7.9 %copy-start.8 = (s32[3]{0:T(128)S(1)}, s32[3]{0:T(128)}, u32[]{:S(2)}) copy-start(s32[3]{0:T(128)} %param.11) | copy-start | bytes 40
  19.9 74.5 %collective-permute-start.4 = (f32[1024,512]{1,0:T(8,128)S(1)}, f32[1024,512]{1,0:T(8,128)}, u32[]{:S(2)}, u32[]{:S(2)}) collective-permute-start(f32[1024,512]{1,0:T(8,128)S(1)} %shard_map.77.refs_3_.refs_0_.refs_5_), channel_id=1, source_target_pairs={{28,0},{0,4},{4,8},{8,12},{12,16},{16,20},{20,24},{24,28},{29,1},{... | collective-permute-start | bytes 6291464 | tf_op jit(solution)/shard_map/ppermute | solution.py:19
  22.6 71.8 %collective-permute-start.6 = (f32[896,512]{1,0:T(8,128)}, f32[896,512]{1,0:T(8,128)}, u32[]{:S(2)}, u32[]{:S(2)}) collective-permute-start(f32[896,512]{1,0:T(8,128)} %slice.13), channel_id=1, source_target_pairs={{3,0},{0,1},{1,2},{2,3},{7,4},{4,5},{5,6},{6,7},{11,8},{8,9},{9,10... | collective-permute-start | bytes 5505032 | tf_op jit(solution)/shard_map/ppermute | solution.py:19
  24.2 70.2 %collective-permute-start.5 = (f32[128,512]{1,0:T(8,128)S(1)}, f32[128,512]{1,0:T(8,128)S(1)}, u32[]{:S(2)}, u32[]{:S(2)}) collective-permute-start(f32[128,512]{1,0:T(8,128)S(1)} %slice.14), channel_id=1, source_target_pairs={{0,1},{1,2},{2,3},{4,5},{5,6},{6,7},{8,9},{9,10},{10,11},{12,13},{... | collective-permute-start | bytes 786440 | tf_op jit(solution)/shard_map/ppermute | solution.py:19
  51.8 1.6 copy-start.1
  53.3 4.8 %copy-start.3 = (bf16[1,1,1536,1024]{3,2,1,0:T(8,128)(2,1)S(1)}, bf16[1,1,1536,1024]{3,2,1,0:T(8,128)(2,1)}, u32[]{:S(2)}) copy-start(bf16[1,1,1536,1024]{3,2,1,0:T(8,128)(2,1)} %param.7) | copy-start | bytes 9437188
  53.3 4.8 %copy-start.5 = (bf16[1,1,1536,1024]{3,2,1,0:T(8,128)(2,1)S(1)}, bf16[1,1,1536,1024]{3,2,1,0:T(8,128)(2,1)}, u32[]{:S(2)}) copy-start(bf16[1,1,1536,1024]{3,2,1,0:T(8,128)(2,1)} %param.8) | copy-start | bytes 9437188
  53.4 4.8 %copy-start.7 = (bf16[512,1024]{1,0:T(8,128)(2,1)S(1)}, bf16[512,1024]{1,0:T(8,128)(2,1)}, u32[]{:S(2)}) copy-start(bf16[512,1024]{1,0:T(8,128)(2,1)} %out_ref.5) | copy-start | bytes 3145732
  56.2 48.3 %collective-permute-start.2 = (f32[1024,512]{1,0:T(8,128)S(1)}, f32[1024,512]{1,0:T(8,128)S(1)}, u32[]{:S(2)}, u32[]{:S(2)}) collective-permute-start(f32[1024,512]{1,0:T(8,128)S(1)} %get-tuple-element.14.x_ref.refs_0_), channel_id=1, source_target_pairs={{28,0},{0,4},{4,8},{8,12},{12,16},{16,20},{20,24},{24,28},{29,1},{... | collective-permute-start | bytes 6291464 | tf_op jit(solution)/shard_map/ppermute | solution.py:19
  58.2 81.2 %collective-permute-start.3 = (f32[1024,512]{1,0:T(8,128)S(1)}, f32[1024,512]{1,0:T(8,128)S(1)}, u32[]{:S(2)}, u32[]{:S(2)}) collective-permute-start(f32[1024,512]{1,0:T(8,128)S(1)} %get-tuple-element.15), channel_id=1, source_target_pairs={{3,0},{0,1},{1,2},{2,3},{7,4},{4,5},{5,6},{6,7},{11,8},{8,9},{9,10... | collective-permute-start | bytes 6291464 | tf_op jit(solution)/shard_map/ppermute | solution.py:19
  97.2 55.9 %collective-permute-start.7 = (f32[1024,512]{1,0:T(8,128)S(1)}, f32[1024,512]{1,0:T(8,128)S(1)}, u32[]{:S(2)}, u32[]{:S(2)}) collective-permute-start(f32[1024,512]{1,0:T(8,128)S(1)} %get-tuple-element.18.refs_3_.own_ref), channel_id=1, source_target_pairs={{28,0},{0,4},{4,8},{8,12},{12,16},{16,20},{20,24},{24,28},{29,1},{... | collective-permute-start | bytes 6291464 | tf_op jit(solution)/shard_map/ppermute | solution.py:19
  98.5 63.3 %collective-permute-start.8 = (f32[512,512]{1,0:T(8,128)S(1)}, f32[512,512]{1,0:T(8,128)S(1)}, u32[]{:S(2)}, u32[]{:S(2)}) collective-permute-start(f32[512,512]{1,0:T(8,128)S(1)} %get-tuple-element.22), channel_id=1, source_target_pairs={{3,0},{0,1},{1,2},{2,3},{7,4},{4,5},{5,6},{6,7},{11,8},{8,9},{9,10... | collective-permute-start | bytes 3145736 | tf_op jit(solution)/shard_map/ppermute | solution.py:19
  102.9 75.8 %collective-permute-start.9 = (f32[384,512]{1,0:T(8,128)S(1)}, f32[384,512]{1,0:T(8,128)S(1)}, u32[]{:S(2)}, u32[]{:S(2)}) collective-permute-start(f32[384,512]{1,0:T(8,128)S(1)} %get-tuple-element.23), channel_id=1, source_target_pairs={{3,0},{0,1},{1,2},{2,3},{7,4},{4,5},{5,6},{6,7},{11,8},{8,9},{9,10... | collective-permute-start | bytes 2359304 | tf_op jit(solution)/shard_map/ppermute | solution.py:19
  104.5 77.0 %collective-permute-start.11 = (f32[128,512]{1,0:T(8,128)S(1)}, f32[128,512]{1,0:T(8,128)S(1)}, u32[]{:S(2)}, u32[]{:S(2)}) collective-permute-start(f32[128,512]{1,0:T(8,128)S(1)} %broadcast_multiply_fusion), channel_id=1, source_target_pairs={{3,1},{7,5},{11,9},{15,13},{19,17},{23,21},{27,25},{31,29}} | collective-permute-start | bytes 786440 | tf_op jit(solution)/shard_map/ppermute | solution.py:24
  139.3 47.1 %collective-permute-start.10 = (f32[128,512]{1,0:T(8,128)S(1)}, f32[128,512]{1,0:T(8,128)S(1)}, u32[]{:S(2)}, u32[]{:S(2)}) collective-permute-start(f32[128,512]{1,0:T(8,128)S(1)} %get-tuple-element.25), channel_id=1, source_target_pairs={{3,0},{0,1},{1,2},{2,3},{7,4},{4,5},{5,6},{6,7},{11,8},{8,9},{9,10... | collective-permute-start | bytes 786440 | tf_op jit(solution)/shard_map/ppermute | solution.py:19

commit v4 on v3

--- a/solution.py
+++ b/solution.py
@@ -1,4 +1,5 @@
 import functools
+import math
 
 import jax
 import jax.numpy as jnp
@@ -85,7 +86,7 @@
         out_shape=jax.ShapeDtypeStruct((width, heads), jnp.float32),
         scratch_shapes=[pltpu.VMEM(current.shape, jnp.bfloat16)],
         compiler_params=pltpu.CompilerParams(
-            dimension_semantics=("arbitrary",), vmem_limit_bytes=20 * 2**20
+            dimension_semantics=("arbitrary",), vmem_limit_bytes=(20 if which else 60) * 2**20
         ),
         cost_estimate=pl.CostEstimate(
             flops=8 * pool * width * heads, bytes_accessed=12 * 2**20, transcendentals=0
@@ -99,7 +100,7 @@
 
 def add_piece(rest, piece, start):
     rows, heads = piece.shape
-    tile = tile_of(rows, 128)
+    tile = tile_of(math.gcd(rows, start), 128)
     first = start // tile
     return pl.pallas_call(
         add_body,

time: 188 us -> 188 us (level)
  local copies, waits for them, and re-layouts: 10.9 us -> 6.41 us
  Pallas kernels: 45.3 us -> 49.1 us
    unnamed x19 -> x15, local copies, waits for them, and re-layouts: 8.93 us -> 2.94 us
    pallas_call x3, Pallas kernels: 26.5 us -> 30.2 us  [local_gradient(): pl.pallas_call(functools.partial(gradient_body, which, tile, width ** (-0...]
  transfers between devices with their start and end apart: 12 -> 12, of which waited for: 6 -> 6; matrix products, arithmetic and copies ran while one was open for 2% -> 3% of each run, Pallas kernels for 24% -> 26%
where the time goes in v4:
time: 188 us; the launch traced here: 187 us
  waiting for transfers between devices  108 us (57%)
  Pallas kernels  49.1 us (26%)
  starting transfers between devices  20 us (11%)
  local copies, waits for them, and re-layouts  6.41 us (3%)
  between operations  2.05 us (1%)
    ppermute x11, waiting for transfers between devices, shifted(): return lax.ppermute(block, axis, route)  108 us
    pallas_call x3, Pallas kernels, local_gradient(): pl.pallas_call(functools.partial(gradient_body, which, tile, width ** (-0...  30.2 us
    ppermute x11, starting transfers between devices, shifted(): return lax.ppermute(block, axis, route)  19.3 us
    pallas_call x3, Pallas kernels, sums(): pl.pallas_call(functools.partial(sums_body, formula, split, cuts, tile),...  8.13 us
    pallas_call x2, Pallas kernels, add_piece(): pl.pallas_call(add_body, grid=(rows // tile,), in_specs=[pl.BlockSpec((ti...  6.25 us
  transfers between devices with their start and end apart: 12, of which 6 were waited for; matrix products, arithmetic and copies ran while one was open for 3% of the time, Pallas kernels for 26%

profile of v4, /device:TPU:0, one launch (start us, length us, event | category | flops | bytes accessed | tf_op | source)
XLA Modules:
  0.0 187.2 jit_solution(17005701405665686920)
XLA Ops:
  1.2 2.6 %collective-permute-start.1 = (f32[1024,512]{1,0:T(8,128)}, f32[1024,512]{1,0:T(8,128)}, u32[]{:S(2)}, u32[]{:S(2)}) collective-permute-start(f32[1024,512]{1,0:T(8,128)} %bitcast.11), channel_id=1, source_target_pairs={{3,0},{0,1},{1,2},{2,3},{7,4},{4,5},{5,6},{6,7},{11,8},{8,9},{9,10... | collective-permute-start | bytes 6291464 | tf_op jit(solution)/shard_map/ppermute | solution.py:20
  3.8 1.3 copy.13
  5.1 12.5 %shard_map.77.refs_3_.refs_0_.refs_5_ = f32[1024,512]{1,0:T(8,128)} custom-call(s32[3,1536]{1,0:T(4,128)} %bitcast.14, f32[1024,512]{1,0:T(8,128)} %bitcast.12, bf16[1536,1024]{1,0:T(8,128)(2,1)} %bitcast.17, bf16[1536,1024]{1,0:T(8,128)(2,1)} %bitcast.20, bf16[512,1024]{1,0:T(8,128)(2,1)} %out_ref.5), custom_call_target="tpu_custom_call" | custom-call | flops 6442450944 | bytes 12582912 | tf_op jit(solution)/shard_map/pallas_call | solution.py:75
  17.6 1.2 collective-permute-start.4
  18.9 2.9 %slice.13 = f32[896,512]{1,0:T(8,128)} slice(f32[1024,512]{1,0:T(8,128)} %shard_map.77.refs_3_.refs_0_.refs_5_), slice={[128:1024], [0:512]} | slice | bytes 3670016 | tf_op jit(solution)/shard_map/slice | solution.py:255
  21.8 1.6 collective-permute-start.6
  23.4 3.5 %collective-permute-start.5 = (f32[128,512]{1,0:T(8,128)S(1)}, f32[128,512]{1,0:T(8,128)S(1)}, u32[]{:S(2)}, u32[]{:S(2)}) collective-permute-start(f32[128,512]{1,0:T(8,128)S(1)} %slice.14), channel_id=1, source_target_pairs={{0,1},{1,2},{2,3},{4,5},{5,6},{6,7},{8,9},{9,10},{10,11},{12,13},{... | collective-permute-start | bytes 786440 | tf_op jit(solution)/shard_map/ppermute | solution.py:20
  26.9 0.7 convert_reduce_fusion
  27.6 0.7 convert_divide_fusion
  28.3 23.4 %collective-permute-done.1.refs_2_ = f32[1024,512]{1,0:T(8,128)} collective-permute-done((f32[1024,512]{1,0:T(8,128)}, f32[1024,512]{1,0:T(8,128)}, u32[]{:S(2)}, u32[]{:S(2)}) %collective-permute-start.1) | collective-permute-done | bytes 2097184 | tf_op jit(solution)/shard_map/ppermute | solution.py:20
  51.8 1.6 copy-done.1
  53.4 2.9 %shard_map.78 = (f32[1024,512]{1,0:T(8,128)S(1)}, f32[1024,512]{1,0:T(8,128)S(1)}) custom-call(f32[4]{0:T(128)S(1)} %pad_maximum_fusion.w_ref, f32[1024,512]{1,0:T(8,128)S(1)} %bitcast.13, f32[1024,512]{1,0:T(8,128)} %collective-permute-done.refs_1_, f32[1024,512]{1,0:T(8,128)} %collective-permute-done.1.refs_2_, f32[1024,512]{1,0:T(8,128)S(1)} %copy-done), custom_call_target="tpu_custom_call" | custom-call | flops 4194304 | bytes 14680064 | tf_op jit(solution)/shard_map/pallas_call | solution.py:192
  56.3 1.9 %collective-permute-start.2 = (f32[1024,512]{1,0:T(8,128)S(1)}, f32[1024,512]{1,0:T(8,128)S(1)}, u32[]{:S(2)}, u32[]{:S(2)}) collective-permute-start(f32[1024,512]{1,0:T(8,128)S(1)} %get-tuple-element.14.x_ref.refs_0_), channel_id=1, source_target_pairs={{28,0},{0,4},{4,8},{8,12},{12,16},{16,20},{20,24},{24,28},{29,1},{... | collective-permute-start | bytes 6291464 | tf_op jit(solution)/shard_map/ppermute | solution.py:20
  58.2 8.9 %shard_map.79.refs_4_.old_ref = f32[1024,512]{1,0:T(8,128)S(1)} custom-call(s32[3,1536]{1,0:T(4,128)S(1)} %bitcast.15, f32[1024,512]{1,0:T(8,128)S(1)} %get-tuple-element.14.x_ref.refs_0_, bf16[1536,1024]{1,0:T(8,128)(2,1)S(1)} %bitcast.18, bf16[1536,1024]{1,0:T(8,128)(2,1)S(1)} %bitcast.21, bf16[512,1024]{1,0:T(8,128)(2,1)S(1)} %copy-done.5), custom_call_target="tpu_custom_call" | custom-call | flops 6442450944 | bytes 12582912 | tf_op jit(solution)/shard_map/pallas_call | solution.py:75
  67.1 27.3 %collective-permute-done.5.refs_2_ = f32[128,512]{1,0:T(8,128)S(1)} collective-permute-done((f32[128,512]{1,0:T(8,128)S(1)}, f32[128,512]{1,0:T(8,128)S(1)}, u32[]{:S(2)}, u32[]{:S(2)}) %collective-permute-start.5) | collective-permute-done | bytes 262176 | tf_op jit(solution)/shard_map/ppermute | solution.py:20
  94.4 2.8 %shard_map.80 = (f32[1024,512]{1,0:T(8,128)S(1)}, f32[512,512]{1,0:T(8,128)S(1)}, f32[384,512]{1,0:T(8,128)S(1)}, f32[128,512]{1,0:T(8,128)S(1)}) custom-call(f32[4]{0:T(128)S(1)} %pad_maximum_fusion.w_ref, f32[1024,512]{1,0:T(8,128)S(1)} %copy-done, f32[1024,512]{1,0:T(8,128)} %collective-permute-done.4.refs_1_, ...), custom_call_target="tpu_custom_call" | custom-call | flops 4194304 | bytes 14680064 | tf_op jit(solution)/shard_map/pallas_call | solution.py:192
  97.2 1.3 collective-permute-start.7
  98.5 2.5 %collective-permute-start.8 = (f32[512,512]{1,0:T(8,128)S(1)}, f32[512,512]{1,0:T(8,128)S(1)}, u32[]{:S(2)}, u32[]{:S(2)}) collective-permute-start(f32[512,512]{1,0:T(8,128)S(1)} %get-tuple-element.22), channel_id=1, source_target_pairs={{3,0},{0,1},{1,2},{2,3},{7,4},{4,5},{5,6},{6,7},{11,8},{8,9},{9,10... | collective-permute-start | bytes 3145736 | tf_op jit(solution)/shard_map/ppermute | solution.py:20
  101.0 0.6 slice.12
  102.9 1.6 collective-permute-start.9
  104.5 0.7 collective-permute-start.11
  105.2 34.1 %collective-permute-done.3.refs_2_ = f32[1024,512]{1,0:T(8,128)S(1)} collective-permute-done((f32[1024,512]{1,0:T(8,128)S(1)}, f32[1024,512]{1,0:T(8,128)S(1)}, u32[]{:S(2)}, u32[]{:S(2)}) %collective-permute-start.3) | collective-permute-done | bytes 2097184 | tf_op jit(solution)/shard_map/ppermute | solution.py:20
  139.3 2.5 %collective-permute-start.10 = (f32[128,512]{1,0:T(8,128)S(1)}, f32[128,512]{1,0:T(8,128)S(1)}, u32[]{:S(2)}, u32[]{:S(2)}) collective-permute-start(f32[128,512]{1,0:T(8,128)S(1)} %get-tuple-element.25), channel_id=1, source_target_pairs={{3,0},{0,1},{1,2},{2,3},{7,4},{4,5},{5,6},{6,7},{11,8},{8,9},{9,10... | collective-permute-start | bytes 786440 | tf_op jit(solution)/shard_map/ppermute | solution.py:20
  141.8 2.5 %shard_map.81 = (f32[1024,512]{1,0:T(8,128)S(1)}, f32[1024,512]{1,0:T(8,128)}) custom-call(f32[4]{0:T(128)S(1)} %pad_maximum_fusion.w_ref, f32[1024,512]{1,0:T(8,128)S(1)} %get-tuple-element.14.x_ref.refs_0_, f32[1024,512]{1,0:T(8,128)S(1)} %collective-permute-done.2.refs_1_, f32[1024,512]{1,0:T(8,128)S(1)} %collective-permute-done.3.refs_2_, ...), custom_call_target="tpu_custom_call" | custom-call | flops 4194304 | bytes 14680064 | tf_op jit(solution)/shard_map/pallas_call | solution.py:192
  144.3 8.8 %shard_map.82.new_ref = f32[1024,512]{1,0:T(8,128)S(1)} custom-call(s32[3,1536]{1,0:T(4,128)S(1)} %bitcast.16, f32[1024,512]{1,0:T(8,128)S(1)} %get-tuple-element.20.x_ref, bf16[1536,1024]{1,0:T(8,128)(2,1)S(1)} %bitcast.19, bf16[1536,1024]{1,0:T(8,128)(2,1)S(1)} %bitcast.22, bf16[512,1024]{1,0:T(8,128)(2,1)S(1)} %copy-done.5), custom_call_target="tpu_custom_call" | custom-call | flops 6442450944 | bytes 12582912 | tf_op jit(solution)/shard_map/pallas_call | solution.py:75
  153.1 3.7 %near.1 = (f32[1024,512]{1,0:T(8,128)}, f32[128,512]{1,0:T(8,128)S(1)}) custom-call(f32[4]{0:T(128)S(1)} %pad_maximum_fusion.w_ref, f32[1024,512]{1,0:T(8,128)S(1)} %get-tuple-element.18.refs_3_.own_ref, f32[1024,512]{1,0:T(8,128)S(1)} %collective-permute-done.7.row_ref, f32[1024,512]{1,0:T(8,128)S(1)} %shard_map.82.new_ref, ...), custom_call_target="tpu_custom_call" | custom-call | flops 4194304 | bytes 12582912 | tf_op jit(solution)/shard_map/near/pallas_call | solution.py:217
  156.9 5.0 %collective-permute-done.8.piece_ref = f32[512,512]{1,0:T(8,128)S(1)} collective-permute-done((f32[512,512]{1,0:T(8,128)S(1)}, f32[512,512]{1,0:T(8,128)S(1)}, u32[]{:S(2)}, u32[]{:S(2)}) %collective-permute-start.8) | collective-permute-done | bytes 1048608 | tf_op jit(solution)/shard_map/ppermute | solution.py:20
  161.8 3.4 %add_piece.2.rest_ref = f32[1024,512]{1,0:T(8,128)} custom-call(f32[1024,512]{1,0:T(8,128)} %get-tuple-element.21.rest_ref, f32[512,512]{1,0:T(8,128)S(1)} %collective-permute-done.8.piece_ref), custom_call_target="tpu_custom_call", output_to_operand_aliasing={{}: (0, {})} | custom-call | flops 524288 | bytes 3145728 | tf_op jit(solution)/shard_map/add_piece/pallas_call | solution.py:105
  165.2 13.5 %collective-permute-done.9.piece_ref = f32[384,512]{1,0:T(8,128)S(1)} collective-permute-done((f32[384,512]{1,0:T(8,128)S(1)}, f32[384,512]{1,0:T(8,128)S(1)}, u32[]{:S(2)}, u32[]{:S(2)}) %collective-permute-start.9) | collective-permute-done | bytes 786464 | tf_op jit(solution)/shard_map/ppermute | solution.py:20
  178.7 2.9 %add_piece.3.filled_ref = f32[1024,512]{1,0:T(8,128)} custom-call(f32[1024,512]{1,0:T(8,128)} %add_piece.2.rest_ref, f32[384,512]{1,0:T(8,128)S(1)} %collective-permute-done.9.piece_ref), custom_call_target="tpu_custom_call", output_to_operand_aliasing={{}: (0, {})} | custom-call | flops 393216 | bytes 2359296 | tf_op jit(solution)/shard_map/add_piece/pallas_call | solution.py:105
  181.5 4.9 %collective-permute-done.10.piece_ref = f32[128,512]{1,0:T(8,128)S(1)} collective-permute-done((f32[128,512]{1,0:T(8,128)S(1)}, f32[128,512]{1,0:T(8,128)S(1)}, u32[]{:S(2)}, u32[]{:S(2)}) %collective-permute-start.10) | collective-permute-done | bytes 262176 | tf_op jit(solution)/shard_map/ppermute | solution.py:20
  186.5 0.8 add_tail.1
  (24 shorter events, 0.7 us)
Async XLA Ops:
  0.6 27.7 %collective-permute-start = (f32[1024,512]{1,0:T(8,128)}, f32[1024,512]{1,0:T(8,128)}, u32[]{:S(2)}, u32[]{:S(2)}) collective-permute-start(f32[1024,512]{1,0:T(8,128)} %bitcast.10), channel_id=1, source_target_pairs={{28,0},{0,4},{4,8},{8,12},{12,16},{16,20},{20,24},{24,28},{29,1},{... | collective-permute-start | bytes 6291464 | tf_op jit(solution)/shard_map/ppermute | solution.py:20
  1.2 50.6 %collective-permute-start.1 = (f32[1024,512]{1,0:T(8,128)}, f32[1024,512]{1,0:T(8,128)}, u32[]{:S(2)}, u32[]{:S(2)}) collective-permute-start(f32[1024,512]{1,0:T(8,128)} %bitcast.11), channel_id=1, source_target_pairs={{3,0},{0,1},{1,2},{2,3},{7,4},{4,5},{5,6},{6,7},{11,8},{8,9},{9,10... | collective-permute-start | bytes 6291464 | tf_op jit(solution)/shard_map/ppermute | solution.py:20
  17.6 4.1 %copy-start = (f32[1024,512]{1,0:T(8,128)S(1)}, f32[1024,512]{1,0:T(8,128)}, u32[]{:S(2)}) copy-start(f32[1024,512]{1,0:T(8,128)} %shard_map.77.refs_3_.refs_0_.refs_5_) | copy-start | bytes 6291460
  17.6 9.3 %copy-start.6 = (s32[3]{0:T(128)S(1)}, s32[3]{0:T(128)}, u32[]{:S(2)}) copy-start(s32[3]{0:T(128)} %param.11) | copy-start | bytes 40
  17.6 76.8 %collective-permute-start.4 = (f32[1024,512]{1,0:T(8,128)}, f32[1024,512]{1,0:T(8,128)}, u32[]{:S(2)}, u32[]{:S(2)}) collective-permute-start(f32[1024,512]{1,0:T(8,128)} %shard_map.77.refs_3_.refs_0_.refs_5_), channel_id=1, source_target_pairs={{28,0},{0,4},{4,8},{8,12},{12,16},{16,20},{20,24},{24,28},{29,1},{... | collective-permute-start | bytes 6291464 | tf_op jit(solution)/shard_map/ppermute | solution.py:20
  21.8 72.6 %collective-permute-start.6 = (f32[896,512]{1,0:T(8,128)}, f32[896,512]{1,0:T(8,128)}, u32[]{:S(2)}, u32[]{:S(2)}) collective-permute-start(f32[896,512]{1,0:T(8,128)} %slice.13), channel_id=1, source_target_pairs={{3,0},{0,1},{1,2},{2,3},{7,4},{4,5},{5,6},{6,7},{11,8},{8,9},{9,10... | collective-permute-start | bytes 5505032 | tf_op jit(solution)/shard_map/ppermute | solution.py:20
  23.4 71.0 %collective-permute-start.5 = (f32[128,512]{1,0:T(8,128)S(1)}, f32[128,512]{1,0:T(8,128)S(1)}, u32[]{:S(2)}, u32[]{:S(2)}) collective-permute-start(f32[128,512]{1,0:T(8,128)S(1)} %slice.14), channel_id=1, source_target_pairs={{0,1},{1,2},{2,3},{4,5},{5,6},{6,7},{8,9},{9,10},{10,11},{12,13},{... | collective-permute-start | bytes 786440 | tf_op jit(solution)/shard_map/ppermute | solution.py:20
  51.8 1.6 copy-start.1
  53.3 4.8 %copy-start.2 = (s32[1,1,3,1536]{3,2,1,0:T(4,128)S(1)}, s32[1,1,3,1536]{3,2,1,0:T(4,128)}, u32[]{:S(2)}) copy-start(s32[1,1,3,1536]{3,2,1,0:T(4,128)} %copy.13) | copy-start | bytes 55300
  53.4 4.8 %copy-start.3 = (bf16[1,1,1536,1024]{3,2,1,0:T(8,128)(2,1)S(1)}, bf16[1,1,1536,1024]{3,2,1,0:T(8,128)(2,1)}, u32[]{:S(2)}) copy-start(bf16[1,1,1536,1024]{3,2,1,0:T(8,128)(2,1)} %param.7) | copy-start | bytes 9437188
  53.4 4.8 %copy-start.4 = (bf16[1,1,1536,1024]{3,2,1,0:T(8,128)(2,1)S(1)}, bf16[1,1,1536,1024]{3,2,1,0:T(8,128)(2,1)}, u32[]{:S(2)}) copy-start(bf16[1,1,1536,1024]{3,2,1,0:T(8,128)(2,1)} %param.8) | copy-start | bytes 9437188
  53.4 4.8 %copy-start.5 = (bf16[512,1024]{1,0:T(8,128)(2,1)S(1)}, bf16[512,1024]{1,0:T(8,128)(2,1)}, u32[]{:S(2)}) copy-start(bf16[512,1024]{1,0:T(8,128)(2,1)} %out_ref.5) | copy-start | bytes 3145732
  56.3 48.3 %collective-permute-start.2 = (f32[1024,512]{1,0:T(8,128)S(1)}, f32[1024,512]{1,0:T(8,128)S(1)}, u32[]{:S(2)}, u32[]{:S(2)}) collective-permute-start(f32[1024,512]{1,0:T(8,128)S(1)} %get-tuple-element.14.x_ref.refs_0_), channel_id=1, source_target_pairs={{28,0},{0,4},{4,8},{8,12},{12,16},{16,20},{20,24},{24,28},{29,1},{... | collective-permute-start | bytes 6291464 | tf_op jit(solution)/shard_map/ppermute | solution.py:20
  58.2 81.2 %collective-permute-start.3 = (f32[1024,512]{1,0:T(8,128)S(1)}, f32[1024,512]{1,0:T(8,128)S(1)}, u32[]{:S(2)}, u32[]{:S(2)}) collective-permute-start(f32[1024,512]{1,0:T(8,128)S(1)} %get-tuple-element.15), channel_id=1, source_target_pairs={{3,0},{0,1},{1,2},{2,3},{7,4},{4,5},{5,6},{6,7},{11,8},{8,9},{9,10... | collective-permute-start | bytes 6291464 | tf_op jit(solution)/shard_map/ppermute | solution.py:20
  97.2 55.9 %collective-permute-start.7 = (f32[1024,512]{1,0:T(8,128)S(1)}, f32[1024,512]{1,0:T(8,128)S(1)}, u32[]{:S(2)}, u32[]{:S(2)}) collective-permute-start(f32[1024,512]{1,0:T(8,128)S(1)} %get-tuple-element.18.refs_3_.own_ref), channel_id=1, source_target_pairs={{28,0},{0,4},{4,8},{8,12},{12,16},{16,20},{20,24},{24,28},{29,1},{... | collective-permute-start | bytes 6291464 | tf_op jit(solution)/shard_map/ppermute | solution.py:20
  98.5 63.3 %collective-permute-start.8 = (f32[512,512]{1,0:T(8,128)S(1)}, f32[512,512]{1,0:T(8,128)S(1)}, u32[]{:S(2)}, u32[]{:S(2)}) collective-permute-start(f32[512,512]{1,0:T(8,128)S(1)} %get-tuple-element.22), channel_id=1, source_target_pairs={{3,0},{0,1},{1,2},{2,3},{7,4},{4,5},{5,6},{6,7},{11,8},{8,9},{9,10... | collective-permute-start | bytes 3145736 | tf_op jit(solution)/shard_map/ppermute | solution.py:20
  102.9 75.8 %collective-permute-start.9 = (f32[384,512]{1,0:T(8,128)S(1)}, f32[384,512]{1,0:T(8,128)S(1)}, u32[]{:S(2)}, u32[]{:S(2)}) collective-permute-start(f32[384,512]{1,0:T(8,128)S(1)} %get-tuple-element.23), channel_id=1, source_target_pairs={{3,0},{0,1},{1,2},{2,3},{7,4},{4,5},{5,6},{6,7},{11,8},{8,9},{9,10... | collective-permute-start | bytes 2359304 | tf_op jit(solution)/shard_map/ppermute | solution.py:20
  104.5 77.0 %collective-permute-start.11 = (f32[128,512]{1,0:T(8,128)S(1)}, f32[128,512]{1,0:T(8,128)S(1)}, u32[]{:S(2)}, u32[]{:S(2)}) collective-permute-start(f32[128,512]{1,0:T(8,128)S(1)} %broadcast_multiply_fusion), channel_id=1, source_target_pairs={{3,1},{7,5},{11,9},{15,13},{19,17},{23,21},{27,25},{31,29}} | collective-permute-start | bytes 786440 | tf_op jit(solution)/shard_map/ppermute | solution.py:25
  139.3 47.1 %collective-permute-start.10 = (f32[128,512]{1,0:T(8,128)S(1)}, f32[128,512]{1,0:T(8,128)S(1)}, u32[]{:S(2)}, u32[]{:S(2)}) collective-permute-start(f32[128,512]{1,0:T(8,128)S(1)} %get-tuple-element.25), channel_id=1, source_target_pairs={{3,0},{0,1},{1,2},{2,3},{7,4},{4,5},{5,6},{6,7},{11,8},{8,9},{9,10... | collective-permute-start | bytes 786440 | tf_op jit(solution)/shard_map/ppermute | solution.py:20
